TPU v7x, 256 devices: a whole 4x4x8 slice. The times are simulated.
256 devices in a mesh: seq: 64 (over x_hi, z, y), tp: 4 (over x_lo, core).
Axes of the slice: x: 4 (x_hi: 2, x_lo: 2; x = x_hi * 2 + x_lo), y: 4, z: 8, core: 2. Of those that a mesh axis runs over, the one named last changes fastest.
Arguments:
- hidden: bfloat16 [8192, 4096], P('seq', 'tp'), may hold values from -6 to 6
- w_proj: bfloat16 [4096, 1024], P('tp'), may hold values from -1 to 1
- codes: int32 [8192, 4], P('seq'), may hold values from 0 to 2047
- embed_table: bfloat16 [3, 2048, 1024], P(None, None, 'tp'), may hold values from -6 to 6
- w_qkv: bfloat16 [1024, 3, 1024], P(None, None, 'tp'), may hold values from -1 to 1
- w_out: bfloat16 [1024, 1024], P('tp'), may hold values from -0.1875 to 0.1875
- head_table: bfloat16 [4, 1024, 2048], P(None, None, 'tp'), may hold values from -1 to 1
- gain_attn: float32 [1024], replicated, may hold values from 0.5 to 1.5
- gain_head: float32 [1024], replicated, may hold values from 0.5 to 1.5
Outputs:
- row_loss: float32 [8192, 4], P('seq')
- grad_hidden: bfloat16 [8192, 4096], P('seq', 'tp')
- grad_proj: float32 [4096, 1024], P('tp', 'seq')
All inputs are finite; a program needn't handle non-finite values.
Results may differ from a plain program's by a relative error of at most 0.02.
Values may be sent and summed in bfloat16 or wider, within the bound.
A program may use at most 64 MiB of HBM per device.

v0:
```python
import jax
import jax.numpy as jnp
from jax import lax
from jax.sharding import PartitionSpec as P

HEADS = 16


def in_blocks(shard, dim, devices):
    before, after = (shard.shape[:dim], shard.shape[dim + 1 :])
    return jnp.moveaxis(shard.reshape(*before, devices, -1, *after), dim, 0)


def sum_at_owner(shard, axis, dim):
    pieces = in_blocks(shard, dim, lax.axis_size(axis))
    arrived = lax.all_to_all(pieces, axis, split_axis=0, concat_axis=0, tiled=True)
    return arrived.astype(jnp.float32).sum(axis=0)


def from_everyone(shard, axis):
    devices = lax.axis_size(axis)
    return lax.all_to_all(
        jnp.broadcast_to(shard[None], (devices, *shard.shape)), axis, 0, 0, tiled=True
    )


def laid_out(pieces, dim):
    pieces = jnp.moveaxis(pieces, 0, dim)
    lengths = pieces.shape
    return pieces.reshape(*lengths[:dim], lengths[dim] * lengths[dim + 1], *lengths[dim + 2 :])


def gather_directly(shard, axis, dim):
    pieces = from_everyone(shard, axis)
    return laid_out(pieces, dim)


def gathered_once(shard, axis):
    leaves = jax.tree.leaves(shard)
    order = sorted(range(len(leaves)), key=lambda k: -leaves[k].size)
    width = (1, *leaves[order[0]].shape)[-1]
    lines = [
        jnp.pad(leaves[k].reshape(-1), (0, -leaves[k].size % width)).reshape(-1, width)
        for k in order
    ]
    both, at, found = (from_everyone(jnp.concatenate(lines), axis), 0, {})
    for k, line in zip(order, lines):
        slab = both[:, at : at + len(line)].reshape(len(both), -1)
        found[k] = slab[:, : leaves[k].size].reshape(-1, *leaves[k].shape)
        at += len(line)
    numbers = iter(range(len(leaves)))
    return jax.tree.map(lambda _: found[next(numbers)], shard)


def joined_by_halves(pieces, combine):
    while len(jax.tree.leaves(pieces)[0]) > 1:
        pieces = jax.vmap(combine)(
            *(jax.tree.map(lambda part: part[side::2], pieces) for side in (0, 1))
        )
    return jax.tree.map(lambda part: part[0], pieces)


def combined_all(shard, axis, combine):
    pieces = gathered_once(shard, axis)
    return joined_by_halves(pieces, combine)


def rms_norm(stream, gain):
    return stream * lax.rsqrt(jnp.mean(stream * stream, axis=-1, keepdims=True) + 1e-06) * gain


def norm_back(stream, gain, cotangent):
    return jax.vjp(lambda value: rms_norm(value, gain), stream)[1](cotangent)[0]


def attend(query, keys, values):
    scale = query.shape[-1] ** (-0.5)
    count = query.shape[1]
    scores = jnp.einsum("fqhd,fkhd->fhqk", query, keys, preferred_element_type=jnp.float32) * scale
    causal = jnp.arange(count)[:, None] >= jnp.arange(count)[None, :]
    scores = jnp.where(causal, scores, -1e30)
    shifted = jnp.exp(scores - jnp.max(scores, axis=-1, keepdims=True))
    weights = shifted / jnp.sum(shifted, axis=-1, keepdims=True)
    weights_low = weights.astype(jnp.bfloat16)
    attended = jnp.einsum(
        "fhqk,fkhd->fqhd", weights_low, values, preferred_element_type=jnp.float32
    ).astype(jnp.bfloat16)
    return (attended, weights, weights_low)


def attend_back(query, keys, values, weights, weights_low, attended_grad):
    scale = query.shape[-1] ** (-0.5)
    prob_grad = jnp.einsum(
        "fqhd,fkhd->fhqk", attended_grad, values, preferred_element_type=jnp.float32
    )
    score_grad = (
        weights * (prob_grad - jnp.sum(weights * prob_grad, axis=-1, keepdims=True)) * scale
    ).astype(jnp.bfloat16)
    query_grad = jnp.einsum(
        "fhqk,fkhd->fqhd", score_grad, keys, preferred_element_type=jnp.float32
    ).astype(jnp.bfloat16)
    key_grad = jnp.einsum(
        "fhqk,fqhd->fkhd", score_grad, query, preferred_element_type=jnp.float32
    ).astype(jnp.bfloat16)
    value_grad = jnp.einsum(
        "fhqk,fqhd->fkhd", weights_low, attended_grad, preferred_element_type=jnp.float32
    ).astype(jnp.bfloat16)
    return jnp.stack([query_grad, key_grad, value_grad], axis=2)


def combine_rows(first, second):
    top = jnp.maximum(first[0], second[0])
    summed = first[1] * jnp.exp(first[0] - top) + second[1] * jnp.exp(second[0] - top)
    return (top, summed, first[2] + second[2])


def body(hidden, w_proj, codes, embed_table, w_qkv, w_out, head_table, gain_attn, gain_head):
    frames = hidden.shape[0]
    width = w_proj.shape[1]
    steps_count = codes.shape[1]
    head_dim = width // HEADS
    local_heads = w_qkv.shape[2] // head_dim
    vocab = embed_table.shape[1]
    vocab_local = head_table.shape[2]
    rank = lax.axis_index("tp")
    total = float(frames * lax.axis_size("seq") * steps_count)
    partial_value = jnp.dot(hidden, w_proj, preferred_element_type=jnp.float32)
    previous = codes[:, : steps_count - 1]
    selector = (previous[..., None] == jnp.arange(vocab, dtype=jnp.int32)).astype(jnp.bfloat16)
    looked = jnp.einsum(
        "fkv,kvd->fkd", selector, embed_table, preferred_element_type=jnp.float32
    ).astype(jnp.bfloat16)
    context = sum_at_owner(partial_value.astype(jnp.bfloat16), "tp", 0)
    looked = lax.all_to_all(looked, "tp", split_axis=0, concat_axis=2, tiled=True)
    row_count = context.shape[0]
    shifted_in = jnp.concatenate(
        [jnp.zeros((row_count, 1, width), jnp.float32), looked.astype(jnp.float32)], axis=1
    )
    stream_in = context[:, None, :] + shifted_in
    normed_in = rms_norm(stream_in, gain_attn).astype(jnp.bfloat16)
    normed_in = gather_directly(normed_in, "tp", 0)
    qkv_local = w_qkv.reshape(width, -1)
    projected = jnp.dot(normed_in.reshape(-1, width), qkv_local, preferred_element_type=jnp.float32)
    projected = projected.astype(jnp.bfloat16).reshape(
        frames, steps_count, 3, local_heads, head_dim
    )
    query, keys, values = (projected[:, :, 0], projected[:, :, 1], projected[:, :, 2])
    attended, weights, weights_low = attend(query, keys, values)
    mixed = jnp.dot(
        attended.reshape(frames * steps_count, -1), w_out, preferred_element_type=jnp.float32
    )
    mixed = mixed.reshape(frames, steps_count, width)
    mixed = sum_at_owner(mixed.astype(jnp.bfloat16), "tp", 0)
    stream_mid = stream_in + mixed
    normed_out = rms_norm(stream_mid, gain_head).astype(jnp.bfloat16)
    normed_out = gather_directly(normed_out, "tp", 0)
    logits = jnp.einsum("fkd,kdv->fkv", normed_out, head_table, preferred_element_type=jnp.float32)
    vocab_ids = jnp.arange(vocab_local, dtype=jnp.int32) + rank * vocab_local
    hits = codes[..., None] == vocab_ids
    target_part = jnp.sum(jnp.where(hits, logits, 0.0), axis=-1)
    local_top = jnp.max(logits, axis=-1)
    exp_local = jnp.sum(jnp.exp(logits - local_top[..., None]), axis=-1)
    top, exp_total, target = combined_all((local_top, exp_local, target_part), "tp", combine_rows)
    log_total = top + jnp.log(exp_total)
    row_loss = log_total - target
    logit_grad = (
        (jnp.exp(logits - log_total[..., None]) - hits.astype(jnp.float32)) / total
    ).astype(jnp.bfloat16)
    normed_part = jnp.einsum(
        "fkv,kdv->fkd", logit_grad, head_table, preferred_element_type=jnp.float32
    )
    normed_grad = sum_at_owner(normed_part.astype(jnp.bfloat16), "tp", 0)
    mid_grad = norm_back(stream_mid, gain_head, normed_grad)
    mid_low = mid_grad.astype(jnp.bfloat16)
    mid_low = gather_directly(mid_low, "tp", 0)
    attended_grad = jnp.dot(mid_low.reshape(-1, width), w_out.T, preferred_element_type=jnp.float32)
    attended_grad = attended_grad.astype(jnp.bfloat16).reshape(
        frames, steps_count, local_heads, head_dim
    )
    qkv_grad = attend_back(query, keys, values, weights, weights_low, attended_grad)
    normin_part = jnp.dot(
        qkv_grad.reshape(frames * steps_count, -1), qkv_local.T, preferred_element_type=jnp.float32
    )
    normin_part = normin_part.reshape(frames, steps_count, width)
    normin_grad = sum_at_owner(normin_part.astype(jnp.bfloat16), "tp", 0)
    stream_grad = mid_grad + norm_back(stream_in, gain_attn, normin_grad)
    context_grad = jnp.sum(stream_grad, axis=1).astype(jnp.bfloat16)
    context_grad = gather_directly(context_grad, "tp", 0)
    grad_hidden = jnp.dot(context_grad, w_proj.T, preferred_element_type=jnp.float32).astype(
        jnp.bfloat16
    )
    term = jnp.dot(hidden.T, context_grad, preferred_element_type=jnp.float32)
    grad_proj = sum_at_owner(term.astype(jnp.bfloat16), "seq", 1)
    return (row_loss, grad_hidden, grad_proj)


def solution(mesh):
    return jax.shard_map(
        body,
        mesh=mesh,
        in_specs=(
            P("seq", "tp"),
            P("tp", None),
            P("seq", None),
            P(None, None, "tp"),
            P(None, None, "tp"),
            P("tp", None),
            P(None, None, "tp"),
            P(),
            P(),
        ),
        out_specs=(P("seq", None), P("seq", "tp"), P("tp", "seq")),
        check_vma=False,
    )
```

profile of v0, /device:TPU:2, one launch (start us, length us, event | category | flops | bytes accessed | tf_op | source)
XLA Modules:
  0.0 275.3 jit_solution(17922993647431794835)
XLA Ops:
  4.8 6.2 %all-to-all-start.1 = ((bf16[128,3,256]{2,1,0:T(4,128)(2,1)}), bf16[128,3,256]{2,1,0:T(4,128)(2,1)}, u32[]{:S(2)}, u32[]{:S(2)}) async-start(bf16[128,3,256]{2,1,0:T(4,128)(2,1)} %copy.37), calls=%async_computation.1 | async-start | bytes 524288 | tf_op jit(solution)/shard_map/all_to_all | solution.py:134
  11.0 2.8 %convolution_convert_fusion.11 = bf16[128,1024]{1,0:T(8,128)(2,1)} fusion(bf16[128,1024]{1,0:T(8,128)(2,1)S(1)} %copy-done.7, bf16[1024,1024]{1,0:T(8,128)(2,1)} %param.10), kind=kOutput, calls=%fused_computation.36 | convolution fusion | flops 268566528 | bytes 2621440 | tf_op jit(solution)/shard_map/dot_general | solution.py:127
  15.5 5.6 %all-to-all-start = ((bf16[4,32,1024]{2,1,0:T(8,128)(2,1)}), bf16[4,32,1024]{2,1,0:T(8,128)(2,1)}, u32[]{:S(2)}, u32[]{:S(2)}) async-start(bf16[4,32,1024]{2,1,0:T(8,128)(2,1)} %bitcast.99), calls=%async_computation | async-start | bytes 524288 | tf_op jit(solution)/shard_map/all_to_all | solution.py:16
  28.4 5.8 %all-to-all-start.2 = ((bf16[4,32,4,1024]{3,2,1,0:T(4,128)(2,1)}), bf16[4,32,4,1024]{3,2,1,0:T(4,128)(2,1)}, u32[]{:S(2)}, u32[]{:S(2)}) async-start(bf16[4,32,4,1024]{3,2,1,0:T(4,128)(2,1)} %broadcast_in_dim.25), calls=%async_computation.2 | async-start | bytes 2097152 | tf_op jit(solution)/shard_map/all_to_all | solution.py:22
  34.3 2.6 copy.40
  36.9 10.3 %all-to-all-done.2 = bf16[4,32,4,1024]{3,2,1,0:T(4,128)(2,1)} async-done(((bf16[4,32,4,1024]{3,2,1,0:T(4,128)(2,1)}), bf16[4,32,4,1024]{3,2,1,0:T(4,128)(2,1)}, u32[]{:S(2)}, u32[]{:S(2)}) %all-to-all-start.2) | async-done | bytes 1048608 | tf_op jit(solution)/shard_map/all_to_all | solution.py:22
  47.2 2.2 reshape_reshape.6
  49.3 3.6 %convolution_convert_fusion.4 = bf16[512,768]{1,0:T(8,128)(2,1)} fusion(bf16[512,1024]{1,0:T(8,128)(2,1)} %reshape_reshape.6, bf16[1024,768]{0,1:T(8,128)(2,1)} %bitcast.90), kind=kOutput, calls=%fused_computation.15 | convolution fusion | flops 805699584 | bytes 3407872 | tf_op jit(solution)/shard_map/dot_general | solution.py:143
  53.0 3.5 %reshape.120 = bf16[128,4,3,4,64]{4,3,2,1,0:T(4,128)(2,1)} reshape(bf16[512,768]{1,0:T(8,128)(2,1)} %convolution_convert_fusion.4) | data formatting | bytes 1572864 | tf_op jit(solution)/shard_map/reshape | solution.py:144
  56.5 2.9 %fusion.48 = (bf16[128,4,1,4,64]{4,3,2,1,0:T(4,128)(2,1)}, bf16[128,4,1,4,64]{4,3,2,1,0:T(4,128)(2,1)}, bf16[128,4,1,4,64]{4,3,2,1,0:T(4,128)(2,1)}) fusion(bf16[128,4,3,4,64]{4,3,2,1,0:T(4,128)(2,1)} %reshape.120), kind=kLoop, calls=%fused_computation.99 | loop fusion | bytes 1572864 | tf_op jit(solution)/shard_map/slice | solution.py:147
  59.4 4.7 %fusion.50 = (f32[128,4,4]{2,1,0:T(4,128)}, f32[128,4,4,4]{2,3,1,0:T(4,128)}) fusion(pred[4,4]{0,1:T(4,128)(4,1)S(1)} %iota_compare_fusion.6, bf16[128,4,1,4,64]{4,3,2,1,0:T(4,128)(2,1)} %get-tuple-element.10, bf16[128,4,1,4,64]{4,3,2,1,0:T(4,128)(2,1)} %get-tuple-element.9), kind=kOutput, calls=%fused_computation.101 | convolution fusion | flops 1081347 | bytes 565264 | tf_op jit(solution)/shard_map/sub | solution.py:82
  64.1 3.0 %fusion.11 = bf16[128,4,4,64]{3,1,2,0:T(4,128)(2,1)} fusion(bf16[128,4,1,4,64]{4,3,2,1,0:T(4,128)(2,1)} %get-tuple-element.11, f32[128,4,4,4]{2,3,1,0:T(4,128)} %get-tuple-element.16, f32[128,4,4]{2,1,0:T(4,128)} %get-tuple-element.15), kind=kOutput, calls=%fused_computation.30 | convolution fusion | flops 1196032 | bytes 565248 | tf_op jit(solution)/shard_map/fhqk,fkhd->fqhd/dot_general | solution.py:85
  67.1 2.2 copy.45
  71.0 16.9 %all_to_all.59 = bf16[4,32,4,1024]{3,1,2,0:T(8,128)(2,1)S(1)} all-to-all(bf16[4,32,4,1024]{3,1,2,0:T(8,128)(2,1)S(1)} %copy.47), channel_id=1, replica_groups=mesh['seq'=64,'tp'=4] {'tp'}, dimensions={0} | all-to-all | bytes 2097152 | tf_op jit(solution)/shard_map/all_to_all | solution.py:16
  90.0 5.8 %all-to-all-start.4 = ((bf16[4,32,4,1024]{3,1,2,0:T(8,128)(2,1)}), bf16[4,32,4,1024]{3,1,2,0:T(8,128)(2,1)}, u32[]{:S(2)}, u32[]{:S(2)}) async-start(bf16[4,32,4,1024]{3,1,2,0:T(8,128)(2,1)} %broadcast_in_dim.29), calls=%async_computation.4 | async-start | bytes 2097152 | tf_op jit(solution)/shard_map/all_to_all | solution.py:22
  95.9 12.9 %all-to-all-done.4 = bf16[4,32,4,1024]{3,1,2,0:T(8,128)(2,1)} async-done(((bf16[4,32,4,1024]{3,1,2,0:T(8,128)(2,1)}), bf16[4,32,4,1024]{3,1,2,0:T(8,128)(2,1)}, u32[]{:S(2)}, u32[]{:S(2)}) %all-to-all-start.4) | async-done | bytes 1048608 | tf_op jit(solution)/shard_map/all_to_all | solution.py:22
  110.1 3.2 %fusion.51 = (f32[128,4]{0,1:T(4,128)S(1)}, f32[128,4,512]{2,0,1:T(8,128)S(1)}) fusion(bf16[128,4,1024]{2,0,1:T(8,128)(2,1)S(1)} %bitcast.89, bf16[4,1024,512]{2,1,0:T(8,128)(2,1)} %param.15), kind=kOutput, calls=%fused_computation.102 | convolution fusion | flops 537132544 | bytes 6293504 | tf_op jit(solution)/shard_map/fkd,kdv->fkv/dot_general | solution.py:157
  113.8 6.1 %all_to_all.60 = f32[4,384,4]{1,2,0:T(4,128)S(1)} all-to-all(f32[4,384,4]{1,2,0:T(4,128)S(1)} %broadcast_in_dim.31), channel_id=1, replica_groups=mesh['seq'=64,'tp'=4] {'tp'}, dimensions={0} | all-to-all | bytes 49152 | tf_op jit(solution)/shard_map/all_to_all | solution.py:22
  122.1 17.2 %all_to_all.61 = bf16[4,32,4,1024]{3,1,2,0:T(8,128)(2,1)S(1)} all-to-all(bf16[4,32,4,1024]{3,1,2,0:T(8,128)(2,1)S(1)} %copy.49), channel_id=1, replica_groups=mesh['seq'=64,'tp'=4] {'tp'}, dimensions={0} | all-to-all | bytes 2097152 | tf_op jit(solution)/shard_map/all_to_all | solution.py:16
  140.9 17.6 %all_to_all.62 = bf16[4,32,4,1024]{3,2,1,0:T(4,128)(2,1)} all-to-all(bf16[4,32,4,1024]{3,2,1,0:T(4,128)(2,1)S(1)} %broadcast_in_dim.33), channel_id=1, replica_groups=mesh['seq'=64,'tp'=4] {'tp'}, dimensions={0} | all-to-all | bytes 2097152 | tf_op jit(solution)/shard_map/all_to_all | solution.py:22
  158.4 2.2 reshape_reshape.7
  160.6 2.5 convolution_convert_fusion.10
  165.2 2.2 fusion.14
  171.3 2.6 pad_maximum_fusion
  173.9 3.7 %copy.54 = bf16[128,4,3,4,64]{0,4,3,2,1:T(8,128)(2,1)} copy(bf16[128,4,3,4,64]{4,1,3,0,2:T(4,128)(2,1)} %pad_maximum_fusion) | data formatting | bytes 1572864 | tf_op jit(solution)/shard_map/stack | solution.py:108
  177.6 2.6 convolution_convert_fusion.1
  180.4 17.0 %all_to_all.63 = bf16[4,32,4,1024]{3,1,2,0:T(8,128)(2,1)S(1)} all-to-all(bf16[4,32,4,1024]{3,1,2,0:T(8,128)(2,1)S(1)} %copy.57), channel_id=1, replica_groups=mesh['seq'=64,'tp'=4] {'tp'}, dimensions={0} | all-to-all | bytes 2097152 | tf_op jit(solution)/shard_map/all_to_all | solution.py:16
  198.1 8.4 %all_to_all.64 = bf16[4,32,1024]{2,1,0:T(8,128)(2,1)S(1)} all-to-all(bf16[4,32,1024]{2,1,0:T(8,128)(2,1)S(1)} %broadcast_in_dim.35), channel_id=1, replica_groups=mesh['seq'=64,'tp'=4] {'tp'}, dimensions={0} | all-to-all | bytes 524288 | tf_op jit(solution)/shard_map/all_to_all | solution.py:22
  208.5 12.5 %all-to-all-start.10 = ((bf16[64,1024,16]{1,2,0:T(8,128)(2,1)}), bf16[64,1024,16]{1,2,0:T(8,128)(2,1)}, u32[]{:S(2)}, u32[]{:S(2)}) async-start(bf16[64,1024,16]{1,2,0:T(8,128)(2,1)} %bitcast.88), calls=%async_computation.10 | async-start | bytes 4194304 | tf_op jit(solution)/shard_map/all_to_all | solution.py:16
  221.1 3.1 %convolution_convert_fusion.9 = bf16[128,1024]{1,0:T(8,128)(2,1)} fusion(bf16[128,1024]{1,0:T(8,128)(2,1)S(1)} %bitcast.97, bf16[1024,1024]{1,0:T(8,128)(2,1)} %param.10), kind=kOutput, calls=%fused_computation.34 | convolution fusion | flops 268566528 | bytes 2621440 | tf_op jit(solution)/shard_map/dot_general | solution.py:189
  224.2 48.5 %all-to-all-done.10 = bf16[64,1024,16]{1,2,0:T(8,128)(2,1)} async-done(((bf16[64,1024,16]{1,2,0:T(8,128)(2,1)}), bf16[64,1024,16]{1,2,0:T(8,128)(2,1)}, u32[]{:S(2)}, u32[]{:S(2)}) %all-to-all-start.10) | async-done | bytes 2097184 | tf_op jit(solution)/shard_map/all_to_all | solution.py:16
  272.7 2.6 convert_reduce_fusion
  (84 shorter events, 31.2 us)
Async XLA Ops:
  0.6 1.9 copy-start
  2.5 8.5 %copy-start.7 = (bf16[128,1024]{1,0:T(8,128)(2,1)S(1)}, bf16[128,1024]{1,0:T(8,128)(2,1)}, u32[]{:S(2)}) copy-start(bf16[128,1024]{1,0:T(8,128)(2,1)} %param.9) | copy-start | bytes 786436
  4.8 10.7 %all-to-all-start.1 = ((bf16[128,3,256]{2,1,0:T(4,128)(2,1)}), bf16[128,3,256]{2,1,0:T(4,128)(2,1)}, u32[]{:S(2)}, u32[]{:S(2)}) async-start(bf16[128,3,256]{2,1,0:T(4,128)(2,1)} %copy.37), calls=%async_computation.1 | async-start | bytes 524288 | tf_op jit(solution)/shard_map/all_to_all | solution.py:134
  11.0 15.7 %copy-start.14 = (f32[1024]{0:T(1024)S(1)}, f32[1024]{0:T(1024)}, u32[]{:S(2)}) copy-start(f32[1024]{0:T(1024)} %param.16) | copy-start | bytes 12292
  15.5 10.1 %all-to-all-start = ((bf16[4,32,1024]{2,1,0:T(8,128)(2,1)}), bf16[4,32,1024]{2,1,0:T(8,128)(2,1)}, u32[]{:S(2)}, u32[]{:S(2)}) async-start(bf16[4,32,1024]{2,1,0:T(8,128)(2,1)} %bitcast.99), calls=%async_computation | async-start | bytes 524288 | tf_op jit(solution)/shard_map/all_to_all | solution.py:16
  28.4 18.7 %all-to-all-start.2 = ((bf16[4,32,4,1024]{3,2,1,0:T(4,128)(2,1)}), bf16[4,32,4,1024]{3,2,1,0:T(4,128)(2,1)}, u32[]{:S(2)}, u32[]{:S(2)}) async-start(bf16[4,32,4,1024]{3,2,1,0:T(4,128)(2,1)} %broadcast_in_dim.25), calls=%async_computation.2 | async-start | bytes 2097152 | tf_op jit(solution)/shard_map/all_to_all | solution.py:22
  71.0 17.9 %copy-start.13 = (f32[1024]{0:T(1024)S(1)}, f32[1024]{0:T(1024)}, u32[]{:S(2)}) copy-start(f32[1024]{0:T(1024)} %param.17) | copy-start | bytes 12292
  88.0 0.8 copy-start.2
  90.0 18.7 %all-to-all-start.4 = ((bf16[4,32,4,1024]{3,1,2,0:T(8,128)(2,1)}), bf16[4,32,4,1024]{3,1,2,0:T(8,128)(2,1)}, u32[]{:S(2)}, u32[]{:S(2)}) async-start(bf16[4,32,4,1024]{3,1,2,0:T(8,128)(2,1)} %broadcast_in_dim.29), calls=%async_computation.4 | async-start | bytes 2097152 | tf_op jit(solution)/shard_map/all_to_all | solution.py:22
  110.1 3.2 %copy-start.15 = (s32[128,4]{0,1:T(4,128)S(1)}, s32[128,4]{0,1:T(4,128)}, u32[]{:S(2)}) copy-start(s32[128,4]{0,1:T(4,128)} %param.11) | copy-start | bytes 6148
  110.1 10.4 %copy-start.1 = (bf16[4,1024,512]{2,1,0:T(8,128)(2,1)S(1)}, bf16[4,1024,512]{2,1,0:T(8,128)(2,1)}, u32[]{:S(2)}) copy-start(bf16[4,1024,512]{2,1,0:T(8,128)(2,1)} %param.15) | copy-start | bytes 12582916
  122.1 17.4 %copy-start.3 = (f32[32,4,1024]{2,0,1:T(8,128)S(1)}, f32[32,4,1024]{2,0,1:T(8,128)}, u32[]{:S(2)}) copy-start(f32[32,4,1024]{2,0,1:T(8,128)} %copy-done.2) | copy-start | bytes 1572868
  139.5 0.8 copy-start.5
  165.2 2.2 copy-start.9
  165.2 2.2 copy-start.12
  167.4 1.2 copy-start.16
  167.4 1.3 copy-start.17
  168.7 1.1 copy-start.11
  168.7 1.8 copy-start.10
  180.4 17.4 %copy-start.4 = (f32[32,4,1024]{2,0,1:T(8,128)S(1)}, f32[32,4,1024]{2,0,1:T(8,128)}, u32[]{:S(2)}) copy-start(f32[32,4,1024]{2,0,1:T(8,128)} %copy-done.2) | copy-start | bytes 1572868
  180.4 17.4 %copy-start.6 = (f32[32,4,1024]{2,0,1:T(8,128)S(1)}, f32[32,4,1024]{2,0,1:T(8,128)}, u32[]{:S(2)}) copy-start(f32[32,4,1024]{2,0,1:T(8,128)} %copy-done.5) | copy-start | bytes 1572868
  197.6 8.9 %copy-start.8 = (bf16[128,1024]{1,0:T(8,128)(2,1)S(1)}, bf16[128,1024]{1,0:T(8,128)(2,1)}, u32[]{:S(2)}) copy-start(bf16[128,1024]{1,0:T(8,128)(2,1)} %param.9) | copy-start | bytes 786436
  208.5 64.2 %all-to-all-start.10 = ((bf16[64,1024,16]{1,2,0:T(8,128)(2,1)}), bf16[64,1024,16]{1,2,0:T(8,128)(2,1)}, u32[]{:S(2)}, u32[]{:S(2)}) async-start(bf16[64,1024,16]{1,2,0:T(8,128)(2,1)} %bitcast.88), calls=%async_computation.10 | async-start | bytes 4194304 | tf_op jit(solution)/shard_map/all_to_all | solution.py:16
where the time goes:
time: 279 us; the launch traced here: 275 us
  blocking collectives  83 us (30%)
  waiting for transfers between devices  75 us (27%)
  matrix products  36.5 us (13%)
  starting transfers between devices  36.1 us (13%)
  local copies, waits for them, and re-layouts  33.3 us (12%)
  other arithmetic  10.3 us (4%)
    all_to_all x3, blocking collectives, sum_at_owner(): lax.all_to_all(pieces, axis, split_axis=0, concat_axis=0, tiled=True)  51 us
    all_to_all x2, waiting for transfers between devices, sum_at_owner(): lax.all_to_all(pieces, axis, split_axis=0, concat_axis=0, tiled=True)  50.1 us
    all_to_all x3, blocking collectives, from_everyone(): lax.all_to_all(jnp.broadcast_to(shard[None], (devices, *shard.shape)), ax...  32 us
    all_to_all x2, waiting for transfers between devices, from_everyone(): lax.all_to_all(jnp.broadcast_to(shard[None], (devices, *shard.shape)), ax...  23.2 us
    all_to_all x2, starting transfers between devices, sum_at_owner(): lax.all_to_all(pieces, axis, split_axis=0, concat_axis=0, tiled=True)  18.2 us
    all_to_all x2, starting transfers between devices, from_everyone(): lax.all_to_all(jnp.broadcast_to(shard[None], (devices, *shard.shape)), ax...  11.7 us
    all_to_all x1, starting transfers between devices, body(): lax.all_to_all(looked, 'tp', split_axis=0, concat_axis=2, tiled=True)  6.24 us
    unnamed x37, local copies, waits for them, and re-layouts  6.19 us
  transfers between devices with their start and end apart: 5, of which 5 were waited for; matrix products, arithmetic and copies ran while one was open for 4% of the time, Pallas kernels for 0%

commit v1 on v0

v1 whole, which is shorter than its diff:
```python
import functools

import jax
import jax.numpy as jnp
from jax import lax
from jax.experimental import pallas as pl
from jax.experimental.pallas import tpu as pltpu
from jax.sharding import PartitionSpec as P

HEADS = 16
KW = 4
TP = 4
EPS = 1e-06
RB = 32
F32 = jnp.float32
BF16 = jnp.bfloat16
MESH = pl.DeviceIdType.MESH
LAYOUT = {64: (2, 8, 4), 4: (1, 2, 2), 1: (1, 1, 1)}


def mm(a, b):
    return jnp.dot(a, b, preferred_element_type=F32)


def mm_t(a, b):
    return lax.dot_general(a, b, (((1,), (1,)), ((), ())), preferred_element_type=F32)


def remote(src, dst, send, recv, device):
    return pltpu.make_async_remote_copy(
        src_ref=src, dst_ref=dst, send_sem=send, recv_sem=recv, device_id=device, device_id_type=MESH
    )


def kernel(
    seq_size,
    hid_h, wproj_h, codes_h, emb_h, wqkv_h, wo_h, head_h, ga_h, gh_h,
    loss_o, ghid_o, gproj_o,
    hg, wproj, codes, emb, wqkv, wo, head, ga, gh,
    ccol, looked, c_s, c_r, c_2, s_in, s_mid, normed, q, k, v, wts, att, bd,
    big, g12, st_c, st, sc, midsum, b_s, b_r, b_s2, b_r2, ag, dkv, dqkv,
    e_s, e_r, e_2, cg, tsend, trecv, psend, precv, part,
    lsem, hid_ss, hid_rs, wo_ss, wo_rs, lk_ss, lk_rs, c_ss, c_rs, att_ss, att_rs,
    st_ss, st_rs, b_ss, b_rs, e_ss, e_rs, t_ss, t_rs, p_ss, p_rs,
):
    xs, zs, ys = LAYOUT[seq_size]
    zb_n = min(2, zs)
    zh_n = zs // zb_n
    npos, nsg = zb_n * ys, xs * zh_n
    cw = 1024 // seq_size
    total = float(128 * seq_size * KW)

    r = lax.axis_index("tp")
    s = lax.axis_index("seq")
    core = r % 2
    chip = r // 2
    p = chip * 2 + (1 - core)
    x = (1 - chip) * 2 + core
    d = (1 - chip) * 2 + (1 - core)
    y = s % ys
    z = (s // ys) % zs
    xh = s // (ys * zs)
    pos = (z % zb_n) * ys + y
    sg = xh * zh_n + z // zb_n
    to_p, to_x, to_d = {"tp": p}, {"tp": x}, {"tp": d}
    flip = {"seq": (xs - 1 - xh) * (ys * zs) + z * ys + y, "tp": x}

    def seq_of(position, supergroup):
        yy, zb = position % ys, position // ys
        zh, xx = supergroup % zh_n, supergroup // zh_n
        return xx * (ys * zs) + (zh * zb_n + zb) * ys + yy

    pos_peers = [lax.rem(pos + i, npos) for i in range(1, npos)]
    sg_peers = [lax.rem(sg + i, nsg) for i in range(1, nsg)]

    def load(src, dst, i):
        copy = pltpu.make_async_copy(src, dst, lsem.at[i])
        copy.start()
        return copy

    l_hid = load(hid_h, hg.at[pos], 0)
    l_wproj = load(wproj_h, wproj, 1)
    l_codes = load(codes_h, codes, 2)
    l_emb = [load(emb_h.at[i], emb.at[i], 3 + i) for i in range(3)]
    l_ga = load(ga_h, ga, 6)
    l_gh = load(gh_h, gh, 7)
    l_qkv = load(wqkv_h, wqkv, 8)
    l_wo = load(wo_h, wo.at[r], 9)
    l_head = load(head_h, head, 10)

    barrier = pltpu.get_barrier_semaphore()
    peers = [to_p, to_x, to_d]
    if xs > 1:
        peers.append(flip)
    peers += [{"seq": seq_of(i, sg)} for i in pos_peers]
    peers += [{"seq": seq_of(pos, i)} for i in sg_peers]
    for peer in peers:
        pl.semaphore_signal(barrier, inc=1, device_id=peer, device_id_type=MESH)

    l_hid.wait()
    l_wproj.wait()
    mine = pl.ds(pl.multiple_of(core * 512, 512), 512)
    other = pl.ds(pl.multiple_of((1 - core) * 512, 512), 512)
    c_s[...] = mm(hg[pos], wproj[:, other]).astype(BF16)

    l_codes.wait()
    st_c[...] = jnp.zeros_like(st_c)
    st_c[0:KW, :] = codes[...].astype(F32)
    code_cols = st_c[...].T
    for i in range(KW):
        ccol[i] = jnp.broadcast_to(code_cols[:, i : i + 1], (128, 128)).astype(jnp.int32)

    pl.semaphore_wait(barrier, len(peers))

    c1 = remote(c_s, c_r, c_ss.at[0], c_rs.at[0], to_p)
    c1.start()

    w_p = remote(wo_h, wo.at[r], wo_ss.at[0], wo_rs.at[r], to_p)
    w_x = remote(wo_h, wo.at[r], wo_ss.at[1], wo_rs.at[r], flip if xs > 1 else to_x)
    w_p.start()
    w_x.start()

    lane = lax.broadcasted_iota(jnp.int32, (128, 128), 1)
    looks = []

    def look(i):
        l_emb[i].wait()
        code = ccol[i]
        hot = jnp.concatenate(
            [(code == lane + 128 * g).astype(F32).astype(BF16) for g in range(16)], axis=1
        )
        looked[r, i] = mm(hot, emb[i]).astype(BF16)
        for n, to in enumerate((to_x, to_p)):
            copy = remote(looked.at[r, i], looked.at[r, i], lk_ss.at[i, n], lk_rs.at[i, r], to)
            copy.start()
            looks.append(copy)

    own_half = mm(hg[pos], wproj[:, mine])
    look(0)
    c1.wait_recv()
    c_2[chip, core] = (own_half + c_r[...].astype(F32)).astype(BF16)
    c2x = remote(c_2.at[chip, core], c_2.at[chip, core], c_ss.at[1], c_rs.at[1], to_x)
    c2p = remote(c_2.at[chip, core], c_2.at[chip, core], c_ss.at[2], c_rs.at[2], to_p)
    c2x.start()
    c2p.start()
    look(1)
    look(2)

    hids = []
    for n in range(1, ys):
        py = lax.rem(y + n, ys)
        copy = remote(hid_h, hg.at[pos], hid_ss.at[n - 1], hid_rs.at[pos], {"seq": seq_of((z % zb_n) * ys + py, sg)})
        copy.start()
        hids.append(copy)
    pos_z = (1 - z % zb_n) * ys + y
    if zb_n > 1:
        copy = remote(hid_h, hg.at[pos], hid_ss.at[3], hid_rs.at[pos], {"seq": seq_of(pos_z, sg)})
        copy.start()
        hids.append(copy)

    bd[...] = (
        lax.broadcasted_iota(jnp.int32, (256, 256), 0) // 64
        == lax.broadcasted_iota(jnp.int32, (256, 256), 1) // 64
    ).astype(F32).astype(BF16)

    relays = []

    def relay(buf, send, recv):
        copy = remote(buf, buf, send, recv, to_p)
        copy.start()
        relays.append(copy)

    def landed(buf, recv):
        remote(buf, buf, lsem.at[15], recv, to_p).wait_recv()

    landed(looked.at[x, 0], lk_rs.at[0, x])
    relay(looked.at[x, 0], lk_ss.at[0, 2], lk_rs.at[0, x + 4])
    landed(c_2.at[1 - chip, core], c_rs.at[1])
    relay(c_2.at[1 - chip, core], c_ss.at[3], c_rs.at[3])
    landed(looked.at[x, 1], lk_rs.at[1, x])
    relay(looked.at[x, 1], lk_ss.at[1, 2], lk_rs.at[1, x + 4])
    landed(c_2.at[chip, 1 - core], c_rs.at[2])
    landed(c_2.at[1 - chip, 1 - core], c_rs.at[3])
    l_ga.wait()

    def stream_rows(i, rb):
        rows = pl.ds(pl.multiple_of(rb * RB, RB), RB)
        ctx = jnp.concatenate(
            [c_2[0, h, rows, :].astype(F32) + c_2[1, h, rows, :].astype(F32) for h in range(2)], axis=1
        )
        if i > 0:
            ctx = ctx + jnp.concatenate([looked[j, i - 1, rows, :].astype(F32) for j in range(TP)], axis=1)
        s_in[i, rows, :] = ctx
        scale = lax.rsqrt(jnp.mean(ctx * ctx, axis=1, keepdims=True) + EPS)
        normed[i, rows, :] = (ctx * scale * ga[...]).astype(BF16)

    def project(i):
        for n, dst in enumerate((q, k, v)):
            dst[i] = mm(normed[i], wqkv[n]).astype(BF16)

    def attend(a):
        probe = [q[a].astype(F32) * k[b].astype(F32) for b in range(a + 1)]
        if a == 0:
            att[r, 0] = v[0]
        else:
            prod = jnp.concatenate(probe, axis=0)
            high = prod.astype(BF16)
            low = (prod - high.astype(F32)).astype(BF16)
            sums = (mm(high, bd[...]) + mm(low, bd[...])) * 0.125
            rows = [sums[b * 128 : (b + 1) * 128] for b in range(a + 1)]
            top = functools.reduce(jnp.maximum, rows)
            rows = [jnp.exp(row - top) for row in rows]
            inv = 1.0 / functools.reduce(jnp.add, rows)
            out = jnp.zeros((128, 256), F32)
            for b in range(a + 1):
                w = rows[b] * inv
                wts[a * (a + 1) // 2 + b] = w
                out = out + w.astype(BF16).astype(F32) * v[b].astype(F32)
            att[r, a] = out.astype(BF16)
        for n, to in enumerate((to_x, to_p)):
            copy = remote(att.at[r, a], att.at[r, a], att_ss.at[a, n], att_rs.at[a, r], to)
            copy.start()
            relays.append(copy)

    for i in range(KW):
        if i > 0:
            if i == 2:
                landed(looked.at[x, 2], lk_rs.at[2, x])
                relay(looked.at[x, 2], lk_ss.at[2, 2], lk_rs.at[2, x + 4])
            landed(looked.at[p, i - 1], lk_rs.at[i - 1, p])
            landed(looked.at[d, i - 1], lk_rs.at[i - 1, d + 4])
        lax.fori_loop(0, 128 // RB, lambda rb, c: (stream_rows(i, rb), c)[1], 0)
        if i == 0:
            l_qkv.wait()
        project(i)
        attend(i)

    if zb_n > 1:
        landed(hg.at[pos_z], hid_rs.at[pos_z])
        for n in range(1, ys):
            py = lax.rem(y + n, ys)
            copy = remote(hg.at[pos_z], hg.at[pos_z], hid_ss.at[3 + n], hid_rs.at[pos_z], {"seq": seq_of((z % zb_n) * ys + py, sg)})
            copy.start()
            hids.append(copy)
    landed(wo.at[x], wo_rs.at[x])
    relay(wo.at[x], wo_ss.at[2], wo_rs.at[x + 4])
    l_wo.wait()
    landed(wo.at[p], wo_rs.at[p])
    l_gh.wait()
    l_head.wait()
    st_c[...] = jnp.zeros_like(st_c)

    def forward(i, carry):
        landed(att.at[x, i], att_rs.at[i, x])
        copy = remote(att.at[x, i], att.at[x, i], att_ss.at[i, 2], att_rs.at[i, x + 4], to_p)
        copy.start()
        acc = s_in[i] + mm(att[r, i], wo[r])
        landed(att.at[p, i], att_rs.at[i, p])
        big[...] = acc + mm(att[p, i], wo[p]) + mm(att[x, i], wo[x])

        @pl.when(i == 0)
        def _():
            landed(wo.at[d], wo_rs.at[d + 4])

        landed(att.at[d, i], att_rs.at[i, d + 4])
        s_mid[i] = big[...] + mm(att[d, i], wo[d])

        def rows_of(rb, c):
            rows = pl.ds(pl.multiple_of(rb * RB, RB), RB)
            val = s_mid[i, rows, :]
            scale = lax.rsqrt(jnp.mean(val * val, axis=1, keepdims=True) + EPS)
            normed[i, rows, :] = (val * scale * gh[...]).astype(BF16)
            return c

        lax.fori_loop(0, 128 // RB, rows_of, 0)
        logits = mm(normed[i], head[i])
        code = ccol[i]
        hit = jnp.concatenate([code == lane + (128 * g + r * 512) for g in range(4)], axis=1)
        top = jnp.max(logits, axis=1, keepdims=True)
        grown = jnp.exp(logits - top)
        total_exp = jnp.sum(grown, axis=1, keepdims=True)
        target = jnp.sum(jnp.where(hit, logits, 0.0), axis=1, keepdims=True)
        st_c[...] = jnp.where(
            lane == i, top, jnp.where(lane == i + 8, total_exp, jnp.where(lane == i + 16, target, st_c[...]))
        )
        pair = jnp.concatenate(
            [jnp.where(hit, 0.0, grown).astype(BF16), hit.astype(F32).astype(BF16)], axis=0
        )
        g12[i] = mm_t(pair, head[i])
        copy.wait_send()
        return carry

    lax.fori_loop(0, KW, forward, 0)

    st[r] = st_c[...].T[0:24, :]
    stats = []
    for n, to in enumerate((to_p, to_x, to_d)):
        copy = remote(st.at[r], st.at[r], st_ss.at[n], st_rs.at[r], to)
        copy.start()
        stats.append(copy)
    for slot in (p, x, d):
        landed(st.at[slot], st_rs.at[slot])
    tops = [st[j, 0:8, :] for j in range(TP)]
    top = functools.reduce(jnp.maximum, tops)
    exp_total = functools.reduce(jnp.add, [st[j, 8:16, :] * jnp.exp(tops[j] - top) for j in range(TP)])
    target = functools.reduce(jnp.add, [st[j, 16:24, :] for j in range(TP)])
    log_total = top + jnp.log(exp_total)
    loss_o[...] = (log_total - target)[0:KW, :]
    sc[...] = jnp.zeros_like(sc)
    sc[0:8, :] = jnp.exp(st[r, 0:8, :] - log_total) * (1.0 / total)
    sc[8:16, :] = (jnp.exp(target - log_total) - 1.0) * (1.0 / total)
    sc[...] = sc[...].T
    midsum[...] = jnp.zeros_like(midsum)

    def send_on(i):
        landed(b_r.at[i], b_rs.at[i, 0])
        b_s2[i] = (ag[i, 1] + b_r[i, 1].astype(F32)).astype(BF16)
        remote(b_s2.at[i], b_r2.at[i], b_ss.at[i, 1], b_rs.at[i, 1], to_x).start()

    def head_back(n, carry):
        i = KW - 1 - n

        def rows_of(rb, c):
            start = pl.multiple_of(rb * RB, RB)
            rows = pl.ds(start, RB)
            ln = lax.broadcasted_iota(jnp.int32, (RB, 128), 1)
            both = sc[rows, :]
            grow = jnp.sum(jnp.where(ln == i, both, 0.0), axis=1, keepdims=True)
            hot = jnp.sum(jnp.where(ln == i + 8, both, 0.0), axis=1, keepdims=True)
            val = s_mid[i, rows, :]
            cot = (grow * g12[i, rows, :] + hot * g12[i, pl.ds(pl.multiple_of(128 + start, RB), RB), :]) * gh[...]
            scale = lax.rsqrt(jnp.mean(val * val, axis=1, keepdims=True) + EPS)
            along = jnp.mean(cot * val, axis=1, keepdims=True) * (scale * scale * scale)
            back = cot * scale - val * along
            midsum[rows, :] = midsum[rows, :] + back
            normed[i, rows, :] = back.astype(BF16)
            return c

        lax.fori_loop(0, 128 // RB, rows_of, 0)
        low = normed[i]
        b_s[i, 0] = mm_t(low, wo[p]).astype(BF16)
        b_s[i, 1] = mm_t(low, wo[d]).astype(BF16)
        remote(b_s.at[i], b_r.at[i], b_ss.at[i, 0], b_rs.at[i, 0], to_p).start()
        ag[i, 1] = mm_t(low, wo[x])
        ag[i, 0] = mm_t(low, wo[r])

        @pl.when(n > 0)
        def _():
            send_on(i + 1)

        return carry

    lax.fori_loop(0, KW, head_back, 0)
    send_on(0)

    for a in range(KW - 1, -1, -1):
        landed(b_r2.at[a], b_rs.at[a, 1])
        out_grad = (ag[a, 0] + b_r[a, 0].astype(F32) + b_r2[a].astype(F32)).astype(BF16).astype(F32)
        if a == 0:
            dq = jnp.zeros((128, 256), F32)
            dk = dkv[0, 0]
            dv = dkv[1, 0] + out_grad
        else:
            prod = jnp.concatenate([out_grad * v[b].astype(F32) for b in range(a + 1)], axis=0)
            high = prod.astype(BF16)
            low = (prod - high.astype(F32)).astype(BF16)
            sums = mm(high, bd[...]) + mm(low, bd[...])
            base = a * (a + 1) // 2
            grads = [sums[b * 128 : (b + 1) * 128] for b in range(a + 1)]
            inner = functools.reduce(jnp.add, [wts[base + b] * grads[b] for b in range(a + 1)])
            dq = jnp.zeros((128, 256), F32)
            for b in range(a + 1):
                w = wts[base + b]
                sgrad = (w * (grads[b] - inner) * 0.125).astype(BF16).astype(F32)
                dq = dq + sgrad * k[b].astype(F32)
                dk_b = sgrad * q[a].astype(F32)
                dv_b = w.astype(BF16).astype(F32) * out_grad
                if a == KW - 1:
                    dkv[0, b] = dk_b
                    dkv[1, b] = dv_b
                else:
                    dkv[0, b] = dkv[0, b] + dk_b
                    dkv[1, b] = dkv[1, b] + dv_b
            dk = dkv[0, a]
            dv = dkv[1, a]
        big[...] = (
            mm_t(dq.astype(BF16), wqkv[0]) + mm_t(dk.astype(BF16), wqkv[1]) + mm_t(dv.astype(BF16), wqkv[2])
        )

        def rows_of(rb, c):
            rows = pl.ds(pl.multiple_of(rb * RB, RB), RB)
            val = s_in[a, rows, :]
            cot = big[rows, :] * ga[...]
            scale = lax.rsqrt(jnp.mean(val * val, axis=1, keepdims=True) + EPS)
            along = jnp.mean(cot * val, axis=1, keepdims=True) * (scale * scale * scale)
            midsum[rows, :] = midsum[rows, :] + cot * scale - val * along
            return c

        lax.fori_loop(0, 128 // RB, rows_of, 0)

    e_s[...] = midsum[:, other].astype(BF16)
    e1 = remote(e_s, e_r, e_ss.at[0], e_rs.at[0], to_p)
    e1.start()
    e1.wait_recv()
    e_2[chip, core] = (midsum[:, mine] + e_r[...].astype(F32)).astype(BF16)
    e2x = remote(e_2.at[chip, core], e_2.at[chip, core], e_ss.at[1], e_rs.at[1], to_x)
    e2p = remote(e_2.at[chip, core], e_2.at[chip, core], e_ss.at[2], e_rs.at[2], to_p)
    e2x.start()
    e2p.start()
    landed(e_2.at[1 - chip, core], e_rs.at[1])
    relay(e_2.at[1 - chip, core], e_ss.at[3], e_rs.at[3])
    landed(e_2.at[chip, 1 - core], e_rs.at[2])
    landed(e_2.at[1 - chip, 1 - core], e_rs.at[3])
    for h in range(2):
        cg[:, h * 512 : (h + 1) * 512] = (e_2[0, h].astype(F32) + e_2[1, h].astype(F32)).astype(BF16)

    for j in range(8):
        block = cg[:, j * 128 : (j + 1) * 128].astype(F32).T.astype(BF16)
        step = min(cw, 128)
        for m in range(128 // step):
            col = j * 128 + m * step
            owner = col // cw
            yy, zz, xx = owner % ys, (owner // ys) % zs, owner // (ys * zs)
            at = (xx * zh_n + zz // zb_n) * cw + col % cw
            tsend[(zz % zb_n) * ys + yy, at : at + step, :] = block[m * step : (m + 1) * step]
    tails = []
    for n, peer in enumerate(pos_peers):
        copy = remote(tsend.at[peer], trecv.at[pos], t_ss.at[n], t_rs.at[pos], {"seq": seq_of(peer, sg)})
        copy.start()
        tails.append(copy)
    trecv[pos] = tsend[pos]

    wproj_rows = 256
    for n in range(1024 // wproj_rows):
        cols = slice(n * wproj_rows, (n + 1) * wproj_rows)
        normed[0, :, cols] = mm_t(cg[...], wproj[cols, :]).astype(BF16)
    o_hid = pltpu.make_async_copy(normed.at[0], ghid_o, lsem.at[11])
    o_hid.start()

    part[...] = mm(trecv[pos], hg[pos])
    for peer in pos_peers:
        landed(hg.at[peer], hid_rs.at[peer]) if zb_n == 1 else None
    if zb_n > 1:
        for n in range(1, npos):
            slot = lax.rem(pos + n, npos)

            @pl.when(slot != pos_z)
            def _():
                landed(hg.at[slot], hid_rs.at[slot])

    for peer in pos_peers:
        landed(trecv.at[peer], t_rs.at[peer])
        part[...] = part[...] + mm(trecv[peer], hg[peer])
    for n in range(nsg):
        psend[n] = part[n * cw : (n + 1) * cw, :].astype(BF16)
    for n, peer in enumerate(sg_peers):
        copy = remote(psend.at[peer], precv.at[sg], p_ss.at[n], p_rs.at[sg], {"seq": seq_of(pos, peer)})
        copy.start()
        tails.append(copy)
    precv[sg] = psend[sg]
    for peer in sg_peers:
        landed(precv.at[peer], p_rs.at[peer])
    gproj_o[...] = functools.reduce(jnp.add, [precv[n].astype(F32) for n in range(nsg)])

    o_hid.wait()
    for copy in (c1, w_p, w_x, c2x, c2p, e1, e2x, e2p, *looks, *hids, *relays, *stats, *tails):
        copy.wait_send()
    for i in range(KW):
        remote(b_s.at[i], b_r.at[i], b_ss.at[i, 0], b_rs.at[i, 0], to_p).wait_send()
        remote(b_s2.at[i], b_r2.at[i], b_ss.at[i, 1], b_rs.at[i, 1], to_x).wait_send()


def body(hidden, w_proj, codes, embed_table, w_qkv, w_out, head_table, gain_attn, gain_head):
    seq_size = lax.axis_size("seq")
    xs, zs, ys = LAYOUT[seq_size]
    npos = min(2, zs) * ys
    nsg = seq_size // npos
    cw = 1024 // seq_size
    vm, dma = pltpu.VMEM, pltpu.SemaphoreType.DMA
    scratch = [
        vm((npos, 128, 1024), BF16), vm((1024, 1024), BF16), vm((KW, 128), jnp.int32),
        vm((3, 2048, 256), BF16), vm((3, 1024, 256), BF16), vm((TP, 256, 1024), BF16),
        vm((KW, 1024, 512), BF16), vm((1, 1024), F32), vm((1, 1024), F32),
        vm((KW, 128, 128), jnp.int32), vm((TP, 3, 128, 256), BF16),
        vm((128, 512), BF16), vm((128, 512), BF16), vm((2, 2, 128, 512), BF16),
        vm((KW, 128, 1024), F32), vm((KW, 128, 1024), F32), vm((KW, 128, 1024), BF16),
        vm((KW, 128, 256), BF16), vm((KW, 128, 256), BF16), vm((KW, 128, 256), BF16),
        vm((10, 128, 256), F32), vm((TP, KW, 128, 256), BF16), vm((256, 256), BF16),
        vm((128, 1024), F32), vm((KW, 256, 1024), F32), vm((128, 128), F32),
        vm((TP, 24, 128), F32), vm((128, 128), F32), vm((128, 1024), F32),
        vm((KW, 2, 128, 256), BF16), vm((KW, 2, 128, 256), BF16), vm((KW, 128, 256), BF16),
        vm((KW, 128, 256), BF16), vm((KW, 2, 128, 256), F32), vm((2, KW, 128, 256), F32),
        vm((8, 128), F32),
        vm((128, 512), BF16), vm((128, 512), BF16), vm((2, 2, 128, 512), BF16), vm((128, 1024), BF16),
        vm((npos, nsg * cw, 128), BF16), vm((npos, nsg * cw, 128), BF16),
        vm((nsg, cw, 1024), BF16), vm((nsg, cw, 1024), BF16), vm((nsg * cw, 1024), F32),
        dma((16,)), dma((8,)), dma((8,)), dma((3,)), dma((8,)), dma((3, 3)), dma((3, 8)),
        dma((4,)), dma((4,)), dma((KW, 3)), dma((KW, 8)), dma((3,)), dma((4,)),
        dma((KW, 2)), dma((KW, 2)), dma((4,)), dma((4,)), dma((8,)), dma((8,)), dma((8,)), dma((8,)),
    ]
    hbm = pl.BlockSpec(memory_space=pl.ANY)
    vmem = pl.BlockSpec(memory_space=pltpu.VMEM)
    loss, grad_hidden, grad_proj = pl.pallas_call(
        functools.partial(kernel, seq_size),
        out_shape=(
            jax.ShapeDtypeStruct((KW, 128), F32),
            jax.ShapeDtypeStruct((128, 1024), BF16),
            jax.ShapeDtypeStruct((cw, 1024), F32),
        ),
        in_specs=[hbm] * 9,
        out_specs=(vmem, hbm, vmem),
        scratch_shapes=scratch,
        compiler_params=pltpu.CompilerParams(
            collective_id=0, has_side_effects=True, vmem_limit_bytes=60 * 2**20
        ),
        name="depth_window",
    )(
        hidden, w_proj, codes.T, embed_table, jnp.transpose(w_qkv, (1, 0, 2)), w_out, head_table,
        gain_attn.reshape(1, -1), gain_head.reshape(1, -1),
    )
    return loss.T, grad_hidden, grad_proj.T


def solution(mesh):
    return jax.shard_map(
        body,
        mesh=mesh,
        in_specs=(
            P("seq", "tp"),
            P("tp", None),
            P("seq", None),
            P(None, None, "tp"),
            P(None, None, "tp"),
            P("tp", None),
            P(None, None, "tp"),
            P(),
            P(),
        ),
        out_specs=(P("seq", None), P("seq", "tp"), P("tp", "seq")),
        check_vma=False,
    )
```

time: 279 us -> 80.6 us (0.29); the launches traced: 275 us -> 80.4 us
  blocking collectives: 83 us -> 0 us
  Pallas kernels: 0 us -> 75.3 us
  waiting for transfers between devices: 75 us -> 0 us
  matrix products: 36.5 us -> 0 us
  starting transfers between devices: 36.1 us -> 0 us
  local copies, waits for them, and re-layouts: 33.3 us -> 4.4 us
  other arithmetic: 10.3 us -> 0 us
    all_to_all x6 -> x0, blocking collectives: 83 us -> none  [the longest x3 51 us: sum_at_owner(): lax.all_to_all(pieces, axis, split_axis=0, concat_axis=0, tiled=True)]
    pallas_call x0 -> x1, Pallas kernels: none -> 75.3 us  [body(): pl.pallas_call(functools.partial(kernel, seq_size), out_shape=(jax.ShapeD...]
    all_to_all x5 -> x0, waiting for transfers between devices: 75 us -> none  [the longest x2 50.1 us: sum_at_owner(): lax.all_to_all(pieces, axis, split_axis=0, concat_axis=0, tiled=True)]
    all_to_all x5 -> x0, starting transfers between devices: 36.1 us -> none  [the longest x2 18.2 us: sum_at_owner(): lax.all_to_all(pieces, axis, split_axis=0, concat_axis=0, tiled=True)]
    dot_general x15 -> x0, matrix products: 31.8 us -> none  [the longest x1 3.64 us: body(): jnp.dot(normed_in.reshape(-1, width), qkv_local, preferred_element_type=j...]
    another operation x3 -> x0, local copies, waits for them, and re-layouts: 8.02 us -> none  [the longest x1 3.7 us: attend_back(): return jnp.stack([query_grad, key_grad, value_grad], axis=2)]
    convert_element_type x6 -> x0, local copies, waits for them, and re-layouts: 6.3 us -> none  [the longest x2 2.85 us: body(): looked.astype(jnp.float32)]
    reshape x5 -> x0, local copies, waits for them, and re-layouts: 5.83 us -> none  [the longest x1 3.51 us: body(): projected.astype(jnp.bfloat16)]
  transfers between devices with their start and end apart: 5 -> 0, of which waited for: 5 -> 0; matrix products, arithmetic and copies ran while one was open for 4% -> 0% of each run, Pallas kernels for 0% -> 0%
where the time goes in v1:
time: 80.6 us; the launch traced here: 80.4 us
  Pallas kernels  75.3 us (93%)
  local copies, waits for them, and re-layouts  4.4 us (5%)
    pallas_call x1, Pallas kernels, body(): pl.pallas_call(functools.partial(kernel, seq_size), out_shape=(jax.ShapeD...  75.3 us
    unnamed x3, local copies, waits for them, and re-layouts  4.4 us

profile of v1, /device:TPU:2, one launch (start us, length us, event | category | flops | bytes accessed | tf_op | source)
XLA Modules:
  0.0 80.4 jit_solution(11488175743587158605)
XLA Ops:
  0.6 75.3 %depth_window.1 = (f32[4,128]{1,0:T(4,128)}, bf16[128,1024]{1,0:T(8,128)(2,1)}, f32[16,1024]{1,0:T(8,128)}) custom-call(bf16[128,1024]{1,0:T(8,128)(2,1)} %hid_h.1, bf16[1024,1024]{1,0:T(8,128)(2,1)} %wproj_h.1, s32[4,128]{1,0:T(4,128)} %bitcast.11, bf16[3,2048,256]{2,1,0:T(8,128)(2,1)} %emb_h.1, bf16[3,1024,256]{2,1,0:T(8,128)(2,1)} %bitcast.6, ...), custom_call_target="tpu_custom_call" | custom-call | tf_op jit(solution)/shard_map/depth_window/pallas_call | solution.py:503
  76.0 1.3 %copy.15 = f32[128,4]{0,1:T(4,128)} copy(f32[128,4]{0,1:T(4,128)} %bitcast.10) | data formatting | bytes 4096
  77.2 1.7 %copy.16 = bf16[128,1024]{1,0:T(8,128)(2,1)} copy(bf16[128,1024]{1,0:T(8,128)(2,1)} %get-tuple-element.13) | data formatting | bytes 524288
  78.9 1.5 %copy.17 = f32[1024,16]{0,1:T(8,128)} copy(f32[1024,16]{0,1:T(8,128)} %bitcast.7) | data formatting | bytes 131072

commit v2 on v1

v2 whole, which is shorter than its diff:
```python
import functools

import jax
import jax.numpy as jnp
from jax import lax
from jax.experimental import pallas as pl
from jax.experimental.pallas import tpu as pltpu
from jax.sharding import PartitionSpec as P

HEADS = 16
KW = 4
TP = 4
EPS = 1e-06
RB = 32
F32 = jnp.float32
BF16 = jnp.bfloat16
MESH = pl.DeviceIdType.MESH
LAYOUT = {64: (2, 8, 4), 8: (2, 2, 2)}


def mm(a, b):
    return jnp.dot(a, b, preferred_element_type=F32)


def mm_t(a, b):
    return lax.dot_general(a, b, (((1,), (1,)), ((), ())), preferred_element_type=F32)


def remote(src, dst, send, recv, device):
    return pltpu.make_async_remote_copy(
        src_ref=src, dst_ref=dst, send_sem=send, recv_sem=recv, device_id=device, device_id_type=MESH
    )


def kernel(
    seq_size,
    hid_h, wproj_h, codes_h, emb_h, wqkv_h, wo_h, head_h, ga_h, gh_h,
    loss_o, ghid_o, gproj_o,
    hg, wproj, codes, emb, wqkv, wo, head, ga, gh,
    ccol, looked, c_s, c_r, c_2, s_in, s_mid, normed, q, k, v, wts, att, bd,
    big, g1, g2, ep, r_in, r_mid, st_c, st, sc, midsum, b_s, b_r, b_s2, b_r2, ag, dkv, dqkv,
    e_s, e_r, e_2, cg, tsend, trecv, psend, precv, part,
    lsem, hid_ss, hid_rs, wo_ss, wo_rs, lk_ss, lk_rs, c_ss, c_rs, att_ss, att_rs,
    st_ss, st_rs, b_ss, b_rs, e_ss, e_rs, t_ss, t_rs, p_ss, p_rs,
):
    xs, zs, ys = LAYOUT[seq_size]
    zb_n = min(2, zs)
    zh_n = zs // zb_n
    npos, nsg = zb_n * ys, xs * zh_n
    cw = 1024 // seq_size
    total = float(128 * seq_size * KW)

    r = lax.axis_index("tp")
    s = lax.axis_index("seq")
    core = r % 2
    chip = r // 2
    p = chip * 2 + (1 - core)
    x = (1 - chip) * 2 + core
    d = (1 - chip) * 2 + (1 - core)
    y = s % ys
    z = (s // ys) % zs
    xh = s // (ys * zs)
    pos = (z % zb_n) * ys + y
    sg = xh * zh_n + z // zb_n
    to_p, to_x, to_d = {"tp": p}, {"tp": x}, {"tp": d}
    flip = {"seq": (xs - 1 - xh) * (ys * zs) + z * ys + y, "tp": x}

    def seq_of(position, supergroup):
        yy, zb = position % ys, position // ys
        zh, xx = supergroup % zh_n, supergroup // zh_n
        return xx * (ys * zs) + (zh * zb_n + zb) * ys + yy

    pos_peers = [lax.rem(pos + i, npos) for i in range(1, npos)]
    sg_peers = [lax.rem(sg + i, nsg) for i in range(1, nsg)]

    def load(src, dst, i):
        copy = pltpu.make_async_copy(src, dst, lsem.at[i])
        copy.start()
        return copy

    l_hid = load(hid_h, hg.at[pos], 0)
    l_wproj = load(wproj_h, wproj, 1)
    l_codes = load(codes_h, codes, 2)
    l_emb = [load(emb_h.at[i], emb.at[i], 3 + i) for i in range(3)]
    l_ga = load(ga_h, ga, 6)
    l_gh = load(gh_h, gh, 7)
    l_qkv = load(wqkv_h, wqkv, 8)
    l_wo = load(wo_h, wo.at[r], 9)
    l_head = load(head_h, head, 10)

    barrier = pltpu.get_barrier_semaphore()
    peers = [to_p, to_x, to_d, flip]
    peers += [{"seq": seq_of(i, sg)} for i in pos_peers]
    peers += [{"seq": seq_of(i, sg), "tp": p} for i in pos_peers]
    peers += [{"seq": seq_of(pos, i)} for i in sg_peers]
    for peer in peers:
        pl.semaphore_signal(barrier, inc=1, device_id=peer, device_id_type=MESH)

    lane = lax.broadcasted_iota(jnp.int32, (128, 128), 1)
    bd[...] = (
        lax.broadcasted_iota(jnp.int32, (256, 256), 0) // 64
        == lax.broadcasted_iota(jnp.int32, (256, 256), 1) // 64
    ).astype(F32).astype(BF16)
    l_codes.wait()
    st_c[...] = jnp.zeros_like(st_c)
    st_c[0:KW, :] = codes[...].astype(F32)
    code_cols = st_c[...].T
    for i in range(KW):
        ccol[i] = jnp.broadcast_to(code_cols[:, i : i + 1], (128, 128)).astype(jnp.int32)
    l_hid.wait()
    l_wproj.wait()
    mine = pl.ds(pl.multiple_of(core * 512, 512), 512)
    other = pl.ds(pl.multiple_of((1 - core) * 512, 512), 512)
    c_s[...] = mm(hg[pos], wproj[:, other]).astype(BF16)
    big[:, 0:512] = mm(hg[pos], wproj[:, mine])
    for i in range(KW - 1):
        l_emb[i].wait()
        code = ccol[i]
        hot = jnp.concatenate(
            [(code == lane + 128 * g).astype(F32).astype(BF16) for g in range(16)], axis=1
        )
        looked[r, i] = mm(hot, emb[i]).astype(BF16)

    pl.semaphore_wait(barrier, len(peers))

    relays = []

    def send(src, dst, ss, rs, to):
        copy = remote(src, dst, ss, rs, to)
        copy.start()
        relays.append(copy)

    def relay(buf, ss, rs):
        send(buf, buf, ss, rs, to_p)

    def landed(buf, recv):
        remote(buf, buf, lsem.at[15], recv, to_p).wait_recv()

    def look(i, n):
        send(looked.at[r, i], looked.at[r, i], lk_ss.at[i, n], lk_rs.at[i, r], (to_x, to_p)[n])

    c1 = remote(c_s, c_r, c_ss.at[0], c_rs.at[0], to_p)
    c1.start()
    look(0, 0)
    c1.wait_recv()
    c_2[chip, core] = (big[:, 0:512] + c_r[...].astype(F32)).astype(BF16)
    send(c_2.at[chip, core], c_2.at[chip, core], c_ss.at[1], c_rs.at[1], to_x)
    send(c_2.at[chip, core], c_2.at[chip, core], c_ss.at[2], c_rs.at[2], to_p)
    look(1, 0)
    look(2, 0)
    look(0, 1)
    look(1, 1)
    look(2, 1)

    send(wo_h, wo.at[r], wo_ss.at[1], wo_rs.at[r], flip)
    send(wo_h, wo.at[r], wo_ss.at[0], wo_rs.at[r], to_p)

    for n in range(1, ys):
        py = lax.rem(y + n, ys)
        send(hid_h, hg.at[pos], hid_ss.at[n - 1], hid_rs.at[pos], {"seq": seq_of((z % zb_n) * ys + py, sg)})
    pos_z = (1 - z % zb_n) * ys + y
    send(hid_h, hg.at[pos], hid_ss.at[3], hid_rs.at[pos], {"seq": seq_of(pos_z, sg)})

    def vocab_hit(i):
        code = ccol[i]
        return jnp.concatenate([code == lane + (128 * g + r * 512) for g in range(4)], axis=1)

    def hot_product(i):
        g2[i] = mm_t(vocab_hit(i).astype(F32).astype(BF16), head[i]).astype(BF16)

    landed(looked.at[x, 0], lk_rs.at[0, x])
    relay(looked.at[x, 0], lk_ss.at[0, 2], lk_rs.at[0, x + 4])
    l_head.wait()
    hot_product(0)
    landed(c_2.at[1 - chip, core], c_rs.at[1])
    relay(c_2.at[1 - chip, core], c_ss.at[3], c_rs.at[3])
    hot_product(1)
    l_ga.wait()
    landed(c_2.at[chip, 1 - core], c_rs.at[2])
    landed(c_2.at[1 - chip, 1 - core], c_rs.at[3])

    def stream_rows(i):
        for rb in range(128 // RB):
            rows = slice(rb * RB, (rb + 1) * RB)
            ctx = jnp.concatenate(
                [c_2[0, h, rows, :].astype(F32) + c_2[1, h, rows, :].astype(F32) for h in range(2)], axis=1
            )
            if i > 0:
                ctx = ctx + jnp.concatenate([looked[j, i - 1, rows, :].astype(F32) for j in range(TP)], axis=1)
            s_in[i, rows, :] = ctx
            scale = lax.rsqrt(jnp.mean(ctx * ctx, axis=1, keepdims=True) + EPS)
            r_in[i, rows, :] = jnp.broadcast_to(scale, (RB, 128))
            normed[i, rows, :] = (ctx * scale * ga[...]).astype(BF16)

    def project(i):
        for n, dst in enumerate((q, k, v)):
            dst[i] = mm(normed[i], wqkv[n]).astype(BF16)

    def attend(a):
        probe = [q[a].astype(F32) * k[b].astype(F32) for b in range(a + 1)]
        if a == 0:
            att[r, 0] = v[0]
        else:
            prod = jnp.concatenate(probe, axis=0)
            high = prod.astype(BF16)
            low = (prod - high.astype(F32)).astype(BF16)
            sums = (mm(high, bd[...]) + mm(low, bd[...])) * 0.125
            rows = [sums[b * 128 : (b + 1) * 128] for b in range(a + 1)]
            top = functools.reduce(jnp.maximum, rows)
            rows = [jnp.exp(row - top) for row in rows]
            inv = 1.0 / functools.reduce(jnp.add, rows)
            out = jnp.zeros((128, 256), F32)
            for b in range(a + 1):
                w = rows[b] * inv
                wts[a * (a + 1) // 2 + b] = w
                out = out + w.astype(BF16).astype(F32) * v[b].astype(F32)
            att[r, a] = out.astype(BF16)
        for n, to in enumerate((to_x, to_p)):
            send(att.at[r, a], att.at[r, a], att_ss.at[a, n], att_rs.at[a, r], to)

    for i in range(KW):
        if i > 0:
            if i > 1:
                landed(looked.at[x, i - 1], lk_rs.at[i - 1, x])
                relay(looked.at[x, i - 1], lk_ss.at[i - 1, 2], lk_rs.at[i - 1, x + 4])
                hot_product(i)
            landed(looked.at[p, i - 1], lk_rs.at[i - 1, p])
            landed(looked.at[d, i - 1], lk_rs.at[i - 1, d + 4])
        stream_rows(i)
        if i == 0:
            l_qkv.wait()
        project(i)
        attend(i)

    landed(hg.at[pos_z], hid_rs.at[pos_z])
    for n in range(1, ys):
        py = lax.rem(y + n, ys)
        send(hg.at[pos_z], hg.at[pos_z], hid_ss.at[3 + n], hid_rs.at[pos_z], {"seq": seq_of((z % zb_n) * ys + py, sg)})
    landed(wo.at[x], wo_rs.at[x])
    relay(wo.at[x], wo_ss.at[2], wo_rs.at[x + 4])
    l_wo.wait()
    landed(wo.at[p], wo_rs.at[p])
    l_gh.wait()
    st_c[...] = jnp.zeros_like(st_c)
    midsum[...] = jnp.zeros_like(midsum)

    def forward(i, carry):
        landed(att.at[x, i], att_rs.at[i, x])
        copy = remote(att.at[x, i], att.at[x, i], att_ss.at[i, 2], att_rs.at[i, x + 4], to_p)
        copy.start()
        acc = s_in[i] + mm(att[r, i], wo[r])
        landed(att.at[p, i], att_rs.at[i, p])
        big[...] = acc + mm(att[p, i], wo[p]) + mm(att[x, i], wo[x])

        @pl.when(i == 0)
        def _():
            landed(wo.at[d], wo_rs.at[d + 4])

        landed(att.at[d, i], att_rs.at[i, d + 4])
        s_mid[i] = big[...] + mm(att[d, i], wo[d])

        for rb in range(128 // RB):
            rows = slice(rb * RB, (rb + 1) * RB)
            val = s_mid[i, rows, :]
            scale = lax.rsqrt(jnp.mean(val * val, axis=1, keepdims=True) + EPS)
            r_mid[i, rows, :] = jnp.broadcast_to(scale, (RB, 128))
            normed[i, rows, :] = (val * scale * gh[...]).astype(BF16)
        logits = mm(normed[i], head[i])
        hit = vocab_hit(i)
        top = jnp.max(logits, axis=1, keepdims=True)
        grown = jnp.exp(logits - top)
        total_exp = jnp.sum(grown, axis=1, keepdims=True)
        target = jnp.sum(jnp.where(hit, logits, 0.0), axis=1, keepdims=True)
        st_c[...] = jnp.where(
            lane == i, top, jnp.where(lane == i + 8, total_exp, jnp.where(lane == i + 16, target, st_c[...]))
        )
        ep[i] = jnp.where(hit, 0.0, grown).astype(BF16)
        copy.wait_send()
        return carry

    lax.fori_loop(0, KW, forward, 0)

    st[r] = st_c[...].T[0:24, :]
    stats = []
    for n, to in enumerate((to_p, to_x, to_d)):
        copy = remote(st.at[r], st.at[r], st_ss.at[n], st_rs.at[r], to)
        copy.start()
        stats.append(copy)
    for i in range(KW):
        g1[i] = mm_t(ep[i], head[i])
    for slot in (p, x, d):
        landed(st.at[slot], st_rs.at[slot])
    tops = [st[j, 0:8, :] for j in range(TP)]
    top = functools.reduce(jnp.maximum, tops)
    exp_total = functools.reduce(jnp.add, [st[j, 8:16, :] * jnp.exp(tops[j] - top) for j in range(TP)])
    target = functools.reduce(jnp.add, [st[j, 16:24, :] for j in range(TP)])
    log_total = top + jnp.log(exp_total)
    loss_o[...] = (log_total - target)[0:KW, :]
    sc[...] = jnp.zeros_like(sc)
    sc[0:8, :] = jnp.exp(st[r, 0:8, :] - log_total) * (1.0 / total)
    sc[8:16, :] = (jnp.exp(target - log_total) - 1.0) * (1.0 / total)
    sc[...] = sc[...].T

    def send_on(i):
        landed(b_r.at[i], b_rs.at[i, 0])
        b_s2[i] = (ag[i, 1] + b_r[i, 1].astype(F32)).astype(BF16)
        remote(b_s2.at[i], b_r2.at[i], b_ss.at[i, 1], b_rs.at[i, 1], to_x).start()

    def head_back(n, carry):
        i = KW - 1 - n

        for rb in range(128 // RB):
            rows = slice(rb * RB, (rb + 1) * RB)
            ln = lax.broadcasted_iota(jnp.int32, (RB, 128), 1)
            both = sc[rows, :]
            grow = jnp.sum(jnp.where(ln == i, both, 0.0), axis=1, keepdims=True)
            hot = jnp.sum(jnp.where(ln == i + 8, both, 0.0), axis=1, keepdims=True)
            val = s_mid[i, rows, :]
            cot = (grow * g1[i, rows, :] + hot * g2[i, rows, :].astype(F32)) * gh[...]
            scale = r_mid[i, rows, 0:1]
            along = jnp.mean(cot * val, axis=1, keepdims=True) * (scale * scale * scale)
            back = cot * scale - val * along
            midsum[rows, :] = midsum[rows, :] + back
            normed[i, rows, :] = back.astype(BF16)

        low = normed[i]
        b_s[i, 0] = mm_t(low, wo[p]).astype(BF16)
        b_s[i, 1] = mm_t(low, wo[d]).astype(BF16)
        remote(b_s.at[i], b_r.at[i], b_ss.at[i, 0], b_rs.at[i, 0], to_p).start()
        ag[i, 1] = mm_t(low, wo[x])
        ag[i, 0] = mm_t(low, wo[r])

        @pl.when(n > 0)
        def _():
            send_on(i + 1)

        return carry

    lax.fori_loop(0, KW, head_back, 0)
    send_on(0)

    for a in range(KW - 1, -1, -1):
        landed(b_r2.at[a], b_rs.at[a, 1])
        out_grad = (ag[a, 0] + b_r[a, 0].astype(F32) + b_r2[a].astype(F32)).astype(BF16).astype(F32)
        if a == 0:
            dq = jnp.zeros((128, 256), F32)
            dk = dkv[0, 0]
            dv = dkv[1, 0] + out_grad
        else:
            prod = jnp.concatenate([out_grad * v[b].astype(F32) for b in range(a + 1)], axis=0)
            high = prod.astype(BF16)
            low = (prod - high.astype(F32)).astype(BF16)
            sums = mm(high, bd[...]) + mm(low, bd[...])
            base = a * (a + 1) // 2
            grads = [sums[b * 128 : (b + 1) * 128] for b in range(a + 1)]
            inner = functools.reduce(jnp.add, [wts[base + b] * grads[b] for b in range(a + 1)])
            dq = jnp.zeros((128, 256), F32)
            for b in range(a + 1):
                w = wts[base + b]
                sgrad = (w * (grads[b] - inner) * 0.125).astype(BF16).astype(F32)
                dq = dq + sgrad * k[b].astype(F32)
                dk_b = sgrad * q[a].astype(F32)
                dv_b = w.astype(BF16).astype(F32) * out_grad
                if a == KW - 1:
                    dkv[0, b] = dk_b
                    dkv[1, b] = dv_b
                else:
                    dkv[0, b] = dkv[0, b] + dk_b
                    dkv[1, b] = dkv[1, b] + dv_b
            dk = dkv[0, a]
            dv = dkv[1, a]
        big[...] = (
            mm_t(dq.astype(BF16), wqkv[0]) + mm_t(dk.astype(BF16), wqkv[1]) + mm_t(dv.astype(BF16), wqkv[2])
        )

        for rb in range(128 // RB):
            rows = slice(rb * RB, (rb + 1) * RB)
            val = s_in[a, rows, :]
            cot = big[rows, :] * ga[...]
            scale = r_in[a, rows, 0:1]
            along = jnp.mean(cot * val, axis=1, keepdims=True) * (scale * scale * scale)
            midsum[rows, :] = midsum[rows, :] + cot * scale - val * along

    e_s[...] = midsum[:, other].astype(BF16)
    e1 = remote(e_s, e_r, e_ss.at[0], e_rs.at[0], to_p)
    e1.start()
    e1.wait_recv()
    e_2[chip, core] = (midsum[:, mine] + e_r[...].astype(F32)).astype(BF16)
    e2x = remote(e_2.at[chip, core], e_2.at[chip, core], e_ss.at[1], e_rs.at[1], to_x)
    e2p = remote(e_2.at[chip, core], e_2.at[chip, core], e_ss.at[2], e_rs.at[2], to_p)
    e2x.start()
    e2p.start()
    landed(e_2.at[1 - chip, core], e_rs.at[1])
    relay(e_2.at[1 - chip, core], e_ss.at[3], e_rs.at[3])

    cg[:, mine] = (e_2[0, core].astype(F32) + e_2[1, core].astype(F32)).astype(BF16)
    for j in range(4):
        block = (
            e_2[0, core, :, j * 128 : (j + 1) * 128].astype(F32) + e_2[1, core, :, j * 128 : (j + 1) * 128].astype(F32)
        ).T.astype(BF16)
        for m in range(128 // cw):
            owner = j * (128 // cw) + m
            yy, zz = owner % ys, owner // ys
            at = (zz // zb_n) * cw
            tsend[(zz % zb_n) * ys + yy, at : at + cw, :] = block[m * cw : (m + 1) * cw]
    for n, peer in enumerate(pos_peers):
        for m, to in enumerate((r, p)):
            send(tsend.at[peer], trecv.at[pos, core], t_ss.at[n, m], t_rs.at[pos, core], {"seq": seq_of(peer, sg), "tp": to})
    send(tsend.at[pos], trecv.at[pos, core], t_ss.at[7, 0], t_rs.at[pos, core], to_p)
    trecv[pos, core] = tsend[pos]

    landed(e_2.at[chip, 1 - core], e_rs.at[2])
    landed(e_2.at[1 - chip, 1 - core], e_rs.at[3])
    cg[:, other] = (e_2[0, 1 - core].astype(F32) + e_2[1, 1 - core].astype(F32)).astype(BF16)
    for n in range(4):
        cols = slice(n * 256, (n + 1) * 256)
        ghid_o[:, cols] = mm_t(cg[...], wproj[cols, :]).astype(BF16)

    for n in range(1, npos):
        slot = lax.rem(pos + n, npos)

        @pl.when(slot != pos_z)
        def _():
            landed(hg.at[slot], hid_rs.at[slot])

    landed(trecv.at[pos, 1 - core], t_rs.at[pos, 1 - core])
    part[...] = mm(trecv[pos].reshape(nsg * cw, 128), hg[pos])
    for peer in pos_peers:
        landed(trecv.at[peer, core], t_rs.at[peer, core])
        landed(trecv.at[peer, 1 - core], t_rs.at[peer, 1 - core])
        part[...] = part[...] + mm(trecv[peer].reshape(nsg * cw, 128), hg[peer])
    for n in range(nsg):
        psend[n] = part[n * cw : (n + 1) * cw, :].astype(BF16)
    for n, peer in enumerate(sg_peers):
        send(psend.at[peer], precv.at[sg], p_ss.at[n], p_rs.at[sg], {"seq": seq_of(pos, peer)})
    precv[sg] = psend[sg]
    for peer in sg_peers:
        landed(precv.at[peer], p_rs.at[peer])
    gproj_o[...] = functools.reduce(jnp.add, [precv[n].astype(F32) for n in range(nsg)])

    for copy in (c1, e1, e2x, e2p, *relays, *stats):
        copy.wait_send()
    for i in range(KW):
        remote(b_s.at[i], b_r.at[i], b_ss.at[i, 0], b_rs.at[i, 0], to_p).wait_send()
        remote(b_s2.at[i], b_r2.at[i], b_ss.at[i, 1], b_rs.at[i, 1], to_x).wait_send()


def hand_out(loss_i, ghid_i, gproj_i, loss_o, ghid_o, gproj_o):
    loss_o[...] = loss_i[...]
    ghid_o[...] = ghid_i[...]
    gproj_o[...] = gproj_i[...]


def body(hidden, w_proj, codes, embed_table, w_qkv, w_out, head_table, gain_attn, gain_head):
    seq_size = lax.axis_size("seq")
    xs, zs, ys = LAYOUT[seq_size]
    npos = min(2, zs) * ys
    nsg = seq_size // npos
    cw = 1024 // seq_size
    vm, dma = pltpu.VMEM, pltpu.SemaphoreType.DMA
    scratch = [
        vm((npos, 128, 1024), BF16), vm((1024, 1024), BF16), vm((KW, 128), jnp.int32),
        vm((3, 2048, 256), BF16), vm((3, 1024, 256), BF16), vm((TP, 256, 1024), BF16),
        vm((KW, 1024, 512), BF16), vm((1, 1024), F32), vm((1, 1024), F32),
        vm((KW, 128, 128), jnp.int32), vm((TP, 3, 128, 256), BF16),
        vm((128, 512), BF16), vm((128, 512), BF16), vm((2, 2, 128, 512), BF16),
        vm((KW, 128, 1024), F32), vm((KW, 128, 1024), F32), vm((KW, 128, 1024), BF16),
        vm((KW, 128, 256), BF16), vm((KW, 128, 256), BF16), vm((KW, 128, 256), BF16),
        vm((10, 128, 256), F32), vm((TP, KW, 128, 256), BF16), vm((256, 256), BF16),
        vm((128, 1024), F32), vm((KW, 128, 1024), F32), vm((KW, 128, 1024), BF16),
        vm((KW, 128, 512), BF16), vm((KW, 128, 128), F32), vm((KW, 128, 128), F32), vm((128, 128), F32),
        vm((TP, 24, 128), F32), vm((128, 128), F32), vm((128, 1024), F32),
        vm((KW, 2, 128, 256), BF16), vm((KW, 2, 128, 256), BF16), vm((KW, 128, 256), BF16),
        vm((KW, 128, 256), BF16), vm((KW, 2, 128, 256), F32), vm((2, KW, 128, 256), F32),
        vm((8, 128), F32),
        vm((128, 512), BF16), vm((128, 512), BF16), vm((2, 2, 128, 512), BF16), vm((128, 1024), BF16),
        vm((npos, nsg * cw // 2, 128), BF16), vm((npos, 2, nsg * cw // 2, 128), BF16),
        vm((nsg, cw, 1024), BF16), vm((nsg, cw, 1024), BF16), vm((nsg * cw, 1024), F32),
        dma((16,)), dma((8,)), dma((8,)), dma((3,)), dma((8,)), dma((3, 3)), dma((3, 8)),
        dma((4,)), dma((4,)), dma((KW, 3)), dma((KW, 8)), dma((3,)), dma((4,)),
        dma((KW, 2)), dma((KW, 2)), dma((4,)), dma((4,)), dma((8, 2)), dma((8, 2)), dma((8,)), dma((8,)),
    ]
    out_shape = (
        jax.ShapeDtypeStruct((KW, 128), F32),
        jax.ShapeDtypeStruct((128, 1024), BF16),
        jax.ShapeDtypeStruct((cw, 1024), F32),
    )
    hbm = pl.BlockSpec(memory_space=pl.ANY)
    vmem = pl.BlockSpec(memory_space=pltpu.VMEM)
    made = pl.pallas_call(
        functools.partial(kernel, seq_size),
        out_shape=out_shape,
        in_specs=[hbm] * 9,
        out_specs=(vmem, vmem, vmem),
        scratch_shapes=scratch,
        compiler_params=pltpu.CompilerParams(
            collective_id=0, has_side_effects=True, vmem_limit_bytes=60 * 2**20
        ),
        name="depth_window",
    )(
        hidden, w_proj, codes.T, embed_table, jnp.transpose(w_qkv, (1, 0, 2)), w_out, head_table,
        gain_attn.reshape(1, -1), gain_head.reshape(1, -1),
    )
    loss, grad_hidden, grad_proj = pl.pallas_call(
        hand_out, out_shape=out_shape, in_specs=[vmem] * 3, out_specs=(vmem,) * 3, name="hand_out"
    )(*made)
    return loss.T, grad_hidden, grad_proj.T


def solution(mesh):
    return jax.shard_map(
        body,
        mesh=mesh,
        in_specs=(
            P("seq", "tp"),
            P("tp", None),
            P("seq", None),
            P(None, None, "tp"),
            P(None, None, "tp"),
            P("tp", None),
            P(None, None, "tp"),
            P(),
            P(),
        ),
        out_specs=(P("seq", None), P("seq", "tp"), P("tp", "seq")),
        check_vma=False,
    )
```

time: 80.6 us -> 73.1 us (0.907)
  local copies, waits for them, and re-layouts: 4.4 us -> 0 us
  Pallas kernels: 75.3 us -> 72.4 us
    unnamed x3 -> x0, local copies, waits for them, and re-layouts: 4.4 us -> none
    pallas_call x1 -> x2, Pallas kernels: 75.3 us -> 72.4 us  [the longest x1 70.7 us: body(): pl.pallas_call(functools.partial(kernel, seq_size), out_shape=out_shape,...]
where the time goes in v2:
time: 73.1 us; the launch traced here: 73 us
  Pallas kernels  72.4 us (99%)
    pallas_call x1, Pallas kernels, body(): pl.pallas_call(functools.partial(kernel, seq_size), out_shape=out_shape,...  70.7 us
    pallas_call x1, Pallas kernels, body(): pl.pallas_call(hand_out, out_shape=out_shape, in_specs=[vmem] * 3, out_sp...  1.69 us

profile of v2, /device:TPU:2, one launch (start us, length us, event | category | flops | bytes accessed | tf_op | source)
XLA Modules:
  0.0 73.0 jit_solution(10526057878356651247)
XLA Ops:
  0.6 70.7 %depth_window.1 = (f32[4,128]{1,0:T(4,128)}, bf16[128,1024]{1,0:T(8,128)(2,1)}, f32[16,1024]{1,0:T(8,128)}) custom-call(bf16[128,1024]{1,0:T(8,128)(2,1)} %hid_h.1, bf16[1024,1024]{1,0:T(8,128)(2,1)} %wproj_h.1, s32[4,128]{1,0:T(4,128)} %bitcast.9, bf16[3,2048,256]{2,1,0:T(8,128)(2,1)} %emb_h.1, bf16[3,1024,256]{2,1,0:T(8,128)(2,1)} %bitcast.6, ...), custom_call_target="tpu_custom_call" | custom-call | tf_op jit(solution)/shard_map/depth_window/pallas_call | solution.py:490
  71.4 1.7 %hand_out.1 = (f32[4,128]{1,0:T(4,128)}, bf16[128,1024]{1,0:T(8,128)(2,1)}, f32[16,1024]{1,0:T(8,128)}) custom-call(f32[4,128]{1,0:T(4,128)} %get-tuple-element.9.loss_i, bf16[128,1024]{1,0:T(8,128)(2,1)} %get-tuple-element.10.ghid_i, f32[16,1024]{1,0:T(8,128)} %get-tuple-element.11.gproj_i), custom_call_target="tpu_custom_call" | custom-call | tf_op jit(solution)/shard_map/hand_out/pallas_call | solution.py:504

commit v3 on v2

--- a/solution.py
+++ b/solution.py
@@ -12,6 +12,7 @@
 TP = 4
 EPS = 1e-06
 RB = 32
+WCUT = 192
 F32 = jnp.float32
 BF16 = jnp.bfloat16
 MESH = pl.DeviceIdType.MESH
@@ -40,7 +41,7 @@
     ccol, looked, c_s, c_r, c_2, s_in, s_mid, normed, q, k, v, wts, att, bd,
     big, g1, g2, ep, r_in, r_mid, st_c, st, sc, midsum, b_s, b_r, b_s2, b_r2, ag, dkv, dqkv,
     e_s, e_r, e_2, cg, tsend, trecv, psend, precv, part,
-    lsem, hid_ss, hid_rs, wo_ss, wo_rs, lk_ss, lk_rs, c_ss, c_rs, att_ss, att_rs,
+    lsem, hid_ss, hid_rs, wo_ss, wo_rs, wo_q, lk_ss, lk_rs, c_ss, c_rs, att_ss, att_rs,
     st_ss, st_rs, b_ss, b_rs, e_ss, e_rs, t_ss, t_rs, p_ss, p_rs,
 ):
     xs, zs, ys = LAYOUT[seq_size]
@@ -70,8 +71,15 @@
         zh, xx = supergroup % zh_n, supergroup // zh_n
         return xx * (ys * zs) + (zh * zb_n + zb) * ys + yy
 
-    pos_peers = [lax.rem(pos + i, npos) for i in range(1, npos)]
-    sg_peers = [lax.rem(sg + i, nsg) for i in range(1, nsg)]
+    def around(size):
+        return sorted(range(size), key=lambda i: -min(i, size - i))
+
+    pos_peers = [
+        lax.rem(z + n, 2) * ys + lax.rem(y + m, ys) for m in around(ys) for n in (1, 0) if n or m
+    ]
+    sg_peers = [
+        lax.rem(xh + n, xs) * zh_n + lax.rem(z // zb_n + m, zh_n) for m in around(zh_n) for n in (1, 0) if n or m
+    ]
 
     def load(src, dst, i):
         copy = pltpu.make_async_copy(src, dst, lsem.at[i])
@@ -113,7 +121,8 @@
     other = pl.ds(pl.multiple_of((1 - core) * 512, 512), 512)
     c_s[...] = mm(hg[pos], wproj[:, other]).astype(BF16)
     big[:, 0:512] = mm(hg[pos], wproj[:, mine])
-    for i in range(KW - 1):
+
+    def look_up(i):
         l_emb[i].wait()
         code = ccol[i]
         hot = jnp.concatenate(
@@ -121,6 +130,8 @@
         )
         looked[r, i] = mm(hot, emb[i]).astype(BF16)
 
+    look_up(0)
+
     pl.semaphore_wait(barrier, len(peers))
 
     relays = []
@@ -139,20 +150,22 @@
     def look(i, n):
         send(looked.at[r, i], looked.at[r, i], lk_ss.at[i, n], lk_rs.at[i, r], (to_x, to_p)[n])
 
+    send(wo_h.at[0:WCUT], wo.at[r, 0:WCUT], wo_ss.at[1], wo_rs.at[r], flip)
     c1 = remote(c_s, c_r, c_ss.at[0], c_rs.at[0], to_p)
     c1.start()
     look(0, 0)
+    look_up(1)
     c1.wait_recv()
     c_2[chip, core] = (big[:, 0:512] + c_r[...].astype(F32)).astype(BF16)
     send(c_2.at[chip, core], c_2.at[chip, core], c_ss.at[1], c_rs.at[1], to_x)
     send(c_2.at[chip, core], c_2.at[chip, core], c_ss.at[2], c_rs.at[2], to_p)
     look(1, 0)
-    look(2, 0)
     look(0, 1)
     look(1, 1)
+    look_up(2)
+    look(2, 0)
     look(2, 1)
-
-    send(wo_h, wo.at[r], wo_ss.at[1], wo_rs.at[r], flip)
+    send(wo_h.at[WCUT:256], wo.at[r, WCUT:256], wo_ss.at[3], wo_q.at[0], to_x)
     send(wo_h, wo.at[r], wo_ss.at[0], wo_rs.at[r], to_p)
 
     for n in range(1, ys):
@@ -236,50 +249,60 @@
     for n in range(1, ys):
         py = lax.rem(y + n, ys)
         send(hg.at[pos_z], hg.at[pos_z], hid_ss.at[3 + n], hid_rs.at[pos_z], {"seq": seq_of((z % zb_n) * ys + py, sg)})
-    landed(wo.at[x], wo_rs.at[x])
-    relay(wo.at[x], wo_ss.at[2], wo_rs.at[x + 4])
     l_wo.wait()
+    for i in range(KW):
+        s_mid[i] = s_in[i] + mm(att[r, i], wo[r])
     landed(wo.at[p], wo_rs.at[p])
+    for i in range(KW):
+        landed(att.at[p, i], att_rs.at[i, p])
+        s_mid[i] = s_mid[i] + mm(att[p, i], wo[p])
+    landed(wo.at[x, 0:WCUT], wo_rs.at[x])
+    relay(wo.at[x, 0:WCUT], wo_ss.at[2], wo_rs.at[x + 4])
+    landed(wo.at[x, WCUT:256], wo_q.at[0])
+    relay(wo.at[x, WCUT:256], wo_ss.at[4], wo_q.at[1])
     l_gh.wait()
-    st_c[...] = jnp.zeros_like(st_c)
     midsum[...] = jnp.zeros_like(midsum)
 
-    def forward(i, carry):
-        landed(att.at[x, i], att_rs.at[i, x])
-        copy = remote(att.at[x, i], att.at[x, i], att_ss.at[i, 2], att_rs.at[i, x + 4], to_p)
-        copy.start()
-        acc = s_in[i] + mm(att[r, i], wo[r])
-        landed(att.at[p, i], att_rs.at[i, p])
-        big[...] = acc + mm(att[p, i], wo[p]) + mm(att[x, i], wo[x])
-
-        @pl.when(i == 0)
-        def _():
-            landed(wo.at[d], wo_rs.at[d + 4])
-
-        landed(att.at[d, i], att_rs.at[i, d + 4])
-        s_mid[i] = big[...] + mm(att[d, i], wo[d])
-
+    def norm_mid(i):
         for rb in range(128 // RB):
             rows = slice(rb * RB, (rb + 1) * RB)
             val = s_mid[i, rows, :]
             scale = lax.rsqrt(jnp.mean(val * val, axis=1, keepdims=True) + EPS)
             r_mid[i, rows, :] = jnp.broadcast_to(scale, (RB, 128))
             normed[i, rows, :] = (val * scale * gh[...]).astype(BF16)
+
+    def heads(i):
         logits = mm(normed[i], head[i])
         hit = vocab_hit(i)
         top = jnp.max(logits, axis=1, keepdims=True)
         grown = jnp.exp(logits - top)
         total_exp = jnp.sum(grown, axis=1, keepdims=True)
         target = jnp.sum(jnp.where(hit, logits, 0.0), axis=1, keepdims=True)
-        st_c[...] = jnp.where(
-            lane == i, top, jnp.where(lane == i + 8, total_exp, jnp.where(lane == i + 16, target, st_c[...]))
-        )
         ep[i] = jnp.where(hit, 0.0, grown).astype(BF16)
-        copy.wait_send()
-        return carry
-
-    lax.fori_loop(0, KW, forward, 0)
-
+        return top, total_exp, target
+
+    found = []
+    for pair in ((0, 1), (2, 3)):
+        for i in pair:
+            landed(att.at[x, i], att_rs.at[i, x])
+            relay(att.at[x, i], att_ss.at[i, 2], att_rs.at[i, x + 4])
+        for i in pair:
+            s_mid[i] = s_mid[i] + mm(att[x, i], wo[x])
+        if pair[0] == 0:
+            landed(wo.at[d, 0:WCUT], wo_rs.at[d + 4])
+            landed(wo.at[d, WCUT:256], wo_q.at[1])
+        for i in pair:
+            landed(att.at[d, i], att_rs.at[i, d + 4])
+        for i in pair:
+            s_mid[i] = s_mid[i] + mm(att[d, i], wo[d])
+        for i in pair:
+            norm_mid(i)
+        found += [heads(i) for i in pair]
+    rows_st = jnp.zeros((128, 128), F32)
+    for i in range(KW):
+        for n in range(3):
+            rows_st = jnp.where(lane == i + 8 * n, found[i][n], rows_st)
+    st_c[...] = rows_st
     st[r] = st_c[...].T[0:24, :]
     stats = []
     for n, to in enumerate((to_p, to_x, to_d)):
@@ -327,13 +350,13 @@
         b_s[i, 0] = mm_t(low, wo[p]).astype(BF16)
         b_s[i, 1] = mm_t(low, wo[d]).astype(BF16)
         remote(b_s.at[i], b_r.at[i], b_ss.at[i, 0], b_rs.at[i, 0], to_p).start()
-        ag[i, 1] = mm_t(low, wo[x])
-        ag[i, 0] = mm_t(low, wo[r])
 
         @pl.when(n > 0)
         def _():
             send_on(i + 1)
 
+        ag[i, 1] = mm_t(low, wo[x])
+        ag[i, 0] = mm_t(low, wo[r])
         return carry
 
     lax.fori_loop(0, KW, head_back, 0)
@@ -476,7 +499,7 @@
         vm((128, 512), BF16), vm((128, 512), BF16), vm((2, 2, 128, 512), BF16), vm((128, 1024), BF16),
         vm((npos, nsg * cw // 2, 128), BF16), vm((npos, 2, nsg * cw // 2, 128), BF16),
         vm((nsg, cw, 1024), BF16), vm((nsg, cw, 1024), BF16), vm((nsg * cw, 1024), F32),
-        dma((16,)), dma((8,)), dma((8,)), dma((3,)), dma((8,)), dma((3, 3)), dma((3, 8)),
+        dma((16,)), dma((8,)), dma((8,)), dma((5,)), dma((8,)), dma((2,)), dma((3, 3)), dma((3, 8)),
         dma((4,)), dma((4,)), dma((KW, 3)), dma((KW, 8)), dma((3,)), dma((4,)),
         dma((KW, 2)), dma((KW, 2)), dma((4,)), dma((4,)), dma((8, 2)), dma((8, 2)), dma((8,)), dma((8,)),
     ]

time: 73.1 us -> 69.7 us (0.953); the launches traced: 73 us -> 68.8 us
  Pallas kernels: 72.4 us -> 68.1 us
    pallas_call x1, Pallas kernels: 70.7 us -> 66.4 us  [body(): pl.pallas_call(functools.partial(kernel, seq_size), out_shape=out_shape,...]
where the time goes in v3:
time: 69.7 us; the launch traced here: 68.8 us
  Pallas kernels  68.1 us (98%)
    pallas_call x1, Pallas kernels, body(): pl.pallas_call(functools.partial(kernel, seq_size), out_shape=out_shape,...  66.4 us
    pallas_call x1, Pallas kernels, body(): pl.pallas_call(hand_out, out_shape=out_shape, in_specs=[vmem] * 3, out_sp...  1.69 us

profile of v3, /device:TPU:2, one launch (start us, length us, event | category | flops | bytes accessed | tf_op | source)
XLA Modules:
  0.0 68.8 jit_solution(18107392323265968262)
XLA Ops:
  0.6 66.4 %depth_window.1 = (f32[4,128]{1,0:T(4,128)}, bf16[128,1024]{1,0:T(8,128)(2,1)}, f32[16,1024]{1,0:T(8,128)}) custom-call(bf16[128,1024]{1,0:T(8,128)(2,1)} %hid_h.1, bf16[1024,1024]{1,0:T(8,128)(2,1)} %wproj_h.1, s32[4,128]{1,0:T(4,128)} %bitcast.9, bf16[3,2048,256]{2,1,0:T(8,128)(2,1)} %emb_h.1, bf16[3,1024,256]{2,1,0:T(8,128)(2,1)} %bitcast.6, ...), custom_call_target="tpu_custom_call" | custom-call | tf_op jit(solution)/shard_map/depth_window/pallas_call | solution.py:513
  67.1 1.7 %hand_out.1 = (f32[4,128]{1,0:T(4,128)}, bf16[128,1024]{1,0:T(8,128)(2,1)}, f32[16,1024]{1,0:T(8,128)}) custom-call(f32[4,128]{1,0:T(4,128)} %get-tuple-element.9.loss_i, bf16[128,1024]{1,0:T(8,128)(2,1)} %get-tuple-element.10.ghid_i, f32[16,1024]{1,0:T(8,128)} %get-tuple-element.11.gproj_i), custom_call_target="tpu_custom_call" | custom-call | tf_op jit(solution)/shard_map/hand_out/pallas_call | solution.py:527

commit v4 on v3

--- a/solution.py
+++ b/solution.py
@@ -329,15 +329,11 @@
         b_s2[i] = (ag[i, 1] + b_r[i, 1].astype(F32)).astype(BF16)
         remote(b_s2.at[i], b_r2.at[i], b_ss.at[i, 1], b_rs.at[i, 1], to_x).start()
 
-    def head_back(n, carry):
-        i = KW - 1 - n
-
+    def head_rows(i):
         for rb in range(128 // RB):
             rows = slice(rb * RB, (rb + 1) * RB)
-            ln = lax.broadcasted_iota(jnp.int32, (RB, 128), 1)
-            both = sc[rows, :]
-            grow = jnp.sum(jnp.where(ln == i, both, 0.0), axis=1, keepdims=True)
-            hot = jnp.sum(jnp.where(ln == i + 8, both, 0.0), axis=1, keepdims=True)
+            grow = sc[rows, i : i + 1]
+            hot = sc[rows, i + 8 : i + 9]
             val = s_mid[i, rows, :]
             cot = (grow * g1[i, rows, :] + hot * g2[i, rows, :].astype(F32)) * gh[...]
             scale = r_mid[i, rows, 0:1]
@@ -346,20 +342,17 @@
             midsum[rows, :] = midsum[rows, :] + back
             normed[i, rows, :] = back.astype(BF16)
 
-        low = normed[i]
-        b_s[i, 0] = mm_t(low, wo[p]).astype(BF16)
-        b_s[i, 1] = mm_t(low, wo[d]).astype(BF16)
+    head_rows(KW - 1)
+    for i in range(KW - 1, -1, -1):
+        b_s[i, 0] = mm_t(normed[i], wo[p]).astype(BF16)
+        b_s[i, 1] = mm_t(normed[i], wo[d]).astype(BF16)
         remote(b_s.at[i], b_r.at[i], b_ss.at[i, 0], b_rs.at[i, 0], to_p).start()
-
-        @pl.when(n > 0)
-        def _():
+        if i < KW - 1:
             send_on(i + 1)
-
-        ag[i, 1] = mm_t(low, wo[x])
-        ag[i, 0] = mm_t(low, wo[r])
-        return carry
-
-    lax.fori_loop(0, KW, head_back, 0)
+        ag[i, 1] = mm_t(normed[i], wo[x])
+        ag[i, 0] = mm_t(normed[i], wo[r])
+        if i > 0:
+            head_rows(i - 1)
     send_on(0)
 
     for a in range(KW - 1, -1, -1):

time: 69.7 us -> 68.5 us (0.983)
  Pallas kernels: 68.1 us -> 67.1 us
    pallas_call x1, Pallas kernels: 66.4 us -> 65.4 us  [body(): pl.pallas_call(functools.partial(kernel, seq_size), out_shape=out_shape,...]
where the time goes in v4:
time: 68.5 us; the launch traced here: 67.8 us
  Pallas kernels  67.1 us (98%)
    pallas_call x1, Pallas kernels, body(): pl.pallas_call(functools.partial(kernel, seq_size), out_shape=out_shape,...  65.4 us
    pallas_call x1, Pallas kernels, body(): pl.pallas_call(hand_out, out_shape=out_shape, in_specs=[vmem] * 3, out_sp...  1.69 us

profile of v4, /device:TPU:2, one launch (start us, length us, event | category | flops | bytes accessed | tf_op | source)
XLA Modules:
  0.0 67.8 jit_solution(13369072985003211057)
XLA Ops:
  0.6 65.4 %depth_window.1 = (f32[4,128]{1,0:T(4,128)}, bf16[128,1024]{1,0:T(8,128)(2,1)}, f32[16,1024]{1,0:T(8,128)}) custom-call(bf16[128,1024]{1,0:T(8,128)(2,1)} %hid_h.1, bf16[1024,1024]{1,0:T(8,128)(2,1)} %wproj_h.1, s32[4,128]{1,0:T(4,128)} %bitcast.9, bf16[3,2048,256]{2,1,0:T(8,128)(2,1)} %emb_h.1, bf16[3,1024,256]{2,1,0:T(8,128)(2,1)} %bitcast.6, ...), custom_call_target="tpu_custom_call" | custom-call | tf_op jit(solution)/shard_map/depth_window/pallas_call | solution.py:506
  66.1 1.7 %hand_out.1 = (f32[4,128]{1,0:T(4,128)}, bf16[128,1024]{1,0:T(8,128)(2,1)}, f32[16,1024]{1,0:T(8,128)}) custom-call(f32[4,128]{1,0:T(4,128)} %get-tuple-element.9.loss_i, bf16[128,1024]{1,0:T(8,128)(2,1)} %get-tuple-element.10.ghid_i, f32[16,1024]{1,0:T(8,128)} %get-tuple-element.11.gproj_i), custom_call_target="tpu_custom_call" | custom-call | tf_op jit(solution)/shard_map/hand_out/pallas_call | solution.py:520
